TPU v7x, 32 devices: a whole 2x2x4 slice. The times are simulated.
32 devices in a mesh: dp: 2 (over x), col: 4 (over z), row: 4 (over y, core).
Axes of the slice: x: 2, y: 2, z: 4, core: 2. Of those that a mesh axis runs over, the one named last changes fastest.
Arguments:
- x_act: bfloat16 [128, 8192], P(('dp', 'row'), 'col'), parts along dimension 0
- ln_gain: float32 [8192], P('col')
- w_in: bfloat16 [8192, 32768], P('row', 'col')
- w_out: bfloat16 [32768, 8192], P('row', 'col')
Outputs:
- output: bfloat16 [128, 8192], P(('dp', 'row'), 'col'), parts along dimension 0
There are 2 independent parts. A program takes and returns all parts, laid end to end along the dimension named above; an argument that names none is the same for every part.
All inputs are finite; a program needn't handle non-finite values.
Results may differ from a plain program's by a relative error of at most 0.00115.
Values are sent between devices in bfloat16 or wider.
A program may use at most 1 GiB of HBM per device.

v0:
```python
import jax
import jax.numpy as jnp
from jax import lax
from jax.sharding import PartitionSpec as P

NORM_EPS = 1e-5


def solution(mesh):
    col_size = mesh.shape["col"]

    def local_block(x_blk, gain_blk, w_in_blk, w_out_blk):
        d_model = x_blk.shape[1] * col_size
        x_f32 = x_blk.astype(jnp.float32)
        part_stats = jnp.stack([jnp.sum(x_f32, axis=1), jnp.sum(x_f32 * x_f32, axis=1)])
        row_stats = lax.psum(part_stats, "col") / d_model
        row_mean = row_stats[0][:, None]
        row_var = row_stats[1][:, None] - row_mean * row_mean
        z_blk = ((x_f32 - row_mean) * lax.rsqrt(row_var + NORM_EPS) * gain_blk).astype(jnp.bfloat16)
        z_rows = lax.all_gather(z_blk, "col", axis=1, tiled=True)
        z_cols = lax.all_to_all(z_rows, "row", 1, 0, tiled=True)
        up_part = jnp.dot(z_cols, w_in_blk, preferred_element_type=jnp.float32)
        up_sum = lax.psum_scatter(up_part, "row", scatter_dimension=0, tiled=True)
        h_blk = jax.nn.gelu(up_sum, approximate=True).astype(jnp.bfloat16)
        h_rows = lax.all_gather(h_blk, "col", axis=1, tiled=True)
        h_cols = lax.all_to_all(h_rows, "row", 1, 0, tiled=True)
        down_part = jnp.dot(h_cols, w_out_blk, preferred_element_type=jnp.float32)
        down_sum = lax.psum_scatter(down_part, "row", scatter_dimension=0, tiled=True)
        return (x_f32 + down_sum).astype(jnp.bfloat16)

    return jax.shard_map(
        local_block,
        mesh=mesh,
        in_specs=(P(("dp", "row"), "col"), P("col"), P("row", "col"), P("row", "col")),
        out_specs=P(("dp", "row"), "col"),
        check_vma=False,
    )
```

profile of v0, /device:TPU:0, one launch (start us, length us, event | category | flops | bytes accessed | tf_op | source)
XLA Modules:
  0.0 178.8 jit_solution(12426020392876078897)
XLA Ops:
  6.5 0.0 reduce-scatter.3.cloned.1.call-start
  6.5 1.0 convert_reduce_fusion
  7.5 13.5 %psum.7 = f32[2,16]{1,0:T(2,128)S(1)} all-reduce(f32[2,16]{1,0:T(2,128)S(1)} %pad_maximum_fusion), channel_id=1, replica_groups=mesh['dp'=2,'col'=4,'row'=4] {'col'}, use_global_device_ids=true, to_apply=%region_2.0 | all-reduce | flops 32 | bytes 256 | tf_op jit(solution)/shard_map/psum | solution.py:16
  21.1 0.9 fusion.11
  22.0 13.8 %all_gather.6 = bf16[16,8192]{1,0:T(8,128)(2,1)S(1)} all-gather(bf16[16,2048]{1,0:T(8,128)(2,1)S(1)} %fusion.11), channel_id=1, replica_groups=mesh['dp'=2,'col'=4,'row'=4] {'col'}, dimensions={1}, use_global_device_ids=true | all-gather | bytes 327680 | tf_op jit(solution)/shard_map/all_gather | solution.py:20
  35.8 8.6 %all_to_all.38 = bf16[16,4,2048]{2,0,1:T(8,128)(2,1)S(1)} all-to-all(bf16[16,4,2048]{2,0,1:T(8,128)(2,1)S(1)} %bitcast.35), channel_id=1, replica_groups=mesh['dp'=2,'col'=4,'row'=4] {'row'}, dimensions={1} | all-to-all | bytes 524288 | tf_op jit(solution)/shard_map/all_to_all | solution.py:21
  44.4 14.9 %fusion.15 = f32[64,8192]{1,0:T(8,128)} fusion(bf16[64,2048]{1,0:T(8,128)(2,1)S(1)} %bitcast.32, bf16[2048,8192]{1,0:T(8,128)(2,1)} %param.6), kind=kOutput, calls=%fused_computation.26 | convolution fusion | flops 2147483648 | bytes 35913728 | tf_op jit(solution)/shard_map/dot_general | solution.py:22
  59.3 0.0 copy-start
  59.3 0.0 reduce-scatter.3.cloned.1.call-update
  59.3 0.0 all-gather.2.cloned.1.call-start
  59.4 28.5 %reduce-scatter.3.cloned.1.call-done = f32[16,8192]{1,0:T(8,128)} async-done(((f32[64,8192]{1,0:T(8,128)}), f32[16,8192]{1,0:T(8,128)}) %reduce-scatter.3.cloned.1.call-update) | async-done | bytes 524304 | tf_op jit(solution)/shard_map/reduce_scatter | solution.py:23
  87.9 1.9 %fusion.7 = bf16[16,8192]{1,0:T(8,128)(2,1)} fusion(f32[16,8192]{1,0:T(8,128)} %reduce-scatter.3.cloned.1.call-done), kind=kLoop, calls=%fused_computation.9 | loop fusion | flops 1179648 | bytes 786432 | tf_op jit(solution)/shard_map/convert_element_type | solution.py:24
  89.8 0.0 all-gather.2.cloned.1.call-update
  89.9 0.0 reduce-scatter.5.cloned.1.call-start
  89.9 28.0 %all-gather.2.cloned.1.call-done = bf16[16,32768]{1,0:T(8,128)(2,1)} async-done(((bf16[16,8192]{1,0:T(8,128)(2,1)}), bf16[16,32768]{1,0:T(8,128)(2,1)}) %all-gather.2.cloned.1.call-update) | async-done | bytes 1048592 | tf_op jit(solution)/shard_map/all_gather | solution.py:25
  117.9 1.3 copy.11
  119.2 17.0 %all_to_all.39 = bf16[16,4,8192]{2,0,1:T(8,128)(2,1)S(1)} all-to-all(bf16[16,4,8192]{2,0,1:T(8,128)(2,1)S(1)} %bitcast.31), channel_id=1, replica_groups=mesh['dp'=2,'col'=4,'row'=4] {'row'}, dimensions={1} | all-to-all | bytes 2097152 | tf_op jit(solution)/shard_map/all_to_all | solution.py:26
  136.2 14.4 %fusion.16 = f32[64,2048]{1,0:T(8,128)} fusion(bf16[64,8192]{1,0:T(8,128)(2,1)S(1)} %bitcast.30, bf16[8192,2048]{1,0:T(8,128)(2,1)} %param.7), kind=kOutput, calls=%fused_computation.27 | convolution fusion | flops 2147483648 | bytes 35127296 | tf_op jit(solution)/shard_map/dot_general | solution.py:27
  150.5 0.0 reduce-scatter.5.cloned.1.call-update
  150.6 20.1 %reduce-scatter.5.cloned.1.call-done = f32[16,2048]{1,0:T(8,128)} async-done(((f32[64,2048]{1,0:T(8,128)}), f32[16,2048]{1,0:T(8,128)}) %reduce-scatter.5.cloned.1.call-update) | async-done | bytes 131088 | tf_op jit(solution)/shard_map/reduce_scatter | solution.py:28
  170.7 0.0 copy-done
  170.7 1.5 fusion.12
  (5 shorter events, 0.0 us)
Async XLA Ops:
  6.5 81.4 %reduce-scatter.3.cloned.1.call-start = ((), (), s32[]{:S(2)}) async-start(), calls=%async_computation.4 | async-start | bytes 2621440 | tf_op jit(solution)/shard_map/reduce_scatter | solution.py:23
  59.3 111.4 %copy-start = (bf16[16,2048]{1,0:T(8,128)(2,1)S(1)}, bf16[16,2048]{1,0:T(8,128)(2,1)}, u32[]{:S(2)}) copy-start(bf16[16,2048]{1,0:T(8,128)(2,1)} %param.4) | copy-start | bytes 196612
  59.3 58.6 %all-gather.2.cloned.1.call-start = ((), (), s32[]{:S(2)}) async-start(), calls=%async_computation.5 | async-start | bytes 1310720 | tf_op jit(solution)/shard_map/all_gather | solution.py:25
  89.9 80.8 %reduce-scatter.5.cloned.1.call-start = ((), (), s32[]{:S(2)}) async-start(), calls=%async_computation.6 | async-start | bytes 655360 | tf_op jit(solution)/shard_map/reduce_scatter | solution.py:28
Sparse Core Ops, SparseCore 0:
  59.5 28.3 reduce-scatter.2
  90.0 27.8 all-gather.1
  150.7 19.9 reduce-scatter.4
where the time goes:
time: 179 us
  waiting for transfers between devices  76.7 us (43%)
  blocking collectives  52.9 us (30%)
  matrix products  29.3 us (16%)
  between operations  13.1 us (7%)
  other arithmetic  5.4 us (3%)
    reduce_scatter x1, waiting for transfers between devices, local_block(): up_sum = lax.psum_scatter(up_part, 'row', scatter_dimension=0, tiled=True)  28.5 us
    all_gather x1, waiting for transfers between devices, local_block(): h_rows = lax.all_gather(h_blk, 'col', axis=1, tiled=True)  28 us
    reduce_scatter x1, waiting for transfers between devices, local_block(): lax.psum_scatter(down_part, 'row', scatter_dimension=0, tiled=True)  20.1 us
    all_to_all x1, blocking collectives, local_block(): h_cols = lax.all_to_all(h_rows, 'row', 1, 0, tiled=True)  17 us
    dot_general x1, matrix products, local_block(): up_part = jnp.dot(z_cols, w_in_blk, preferred_element_type=jnp.float32)  14.9 us
    dot_general x1, matrix products, local_block(): down_part = jnp.dot(h_cols, w_out_blk, preferred_element_type=jnp.float32)  14.4 us
    all_gather x1, blocking collectives, local_block(): z_rows = lax.all_gather(z_blk, 'col', axis=1, tiled=True)  13.8 us
    psum x1, blocking collectives, local_block(): row_stats = lax.psum(part_stats, 'col') / d_model  13.5 us
  transfers between devices with their start and end apart: 3, of which 3 were waited for; matrix products, arithmetic and copies ran while one was open for 0% of the time, Pallas kernels for 0%

commit v1 on v0

v1 whole, which is shorter than its diff:
```python
import functools

import jax
import jax.numpy as jnp
from jax import lax
from jax.experimental import pallas as pl
from jax.experimental.pallas import tpu as pltpu
from jax.sharding import PartitionSpec as P

NORM_EPS = 1e-5
MESH = pl.DeviceIdType.MESH
BF16, F32 = jnp.bfloat16, jnp.float32
N_COL = 4
N_ROW = 4


def gelu_tanh(x):
    return x * (0.5 * (1.0 + jnp.tanh(0.7978845608028654 * (x + 0.044715 * (x * x * x)))))


def mlp_kernel(
    n_chunks, n_slots, blk,
    x_hbm, g_hbm, w_in_hbm, w_out_hbm, y_ref,
    x_own, gain, stats, x_all, z_ref, ring, part, from_near, from_far, hid, acc, near_sum, pair_sum, far_sum,
    x_load, w_load, x_send, x_recv, g_send, g_recv, s_send, s_recv, p_send, p_recv, f_recv,
    h_up, h_down, h_recv, n_send, n_recv, o_send, o_recv,
):
    dp, c, r = lax.axis_index("dp"), lax.axis_index("col"), lax.axis_index("row")
    rows = x_own.shape[0]
    n_blk = x_own.shape[1] // blk
    d_model = x_own.shape[1] * N_COL
    near = r + 1 - 2 * (r % 2)
    far = (r + 2) % N_ROW
    me = c * N_ROW + r
    is_root = c == r

    def remote(src, dst, send, recv, to_col, to_row):
        return pltpu.make_async_remote_copy(
            src_ref=src, dst_ref=dst, send_sem=send, recv_sem=recv,
            device_id=(dp, to_col, to_row), device_id_type=MESH,
        )

    def peer(i):
        other = (me + i) % (N_COL * N_ROW)
        return other // N_ROW, other % N_ROW

    x_cp = pltpu.make_async_copy(x_hbm, x_own, x_load.at[0])
    x_cp.start()
    g_cp = pltpu.make_async_copy(g_hbm, gain.at[c], x_load.at[1])
    g_cp.start()
    barrier = pltpu.get_barrier_semaphore()
    for i in range(1, N_COL * N_ROW):
        pc, pr = peer(i)
        pl.semaphore_signal(barrier, inc=1, device_id=(dp, pc, pr), device_id_type=MESH)

    def load_in(j, slot):
        for k in range(n_blk):
            pltpu.make_async_copy(
                w_in_hbm.at[pl.ds(k * blk, blk), pl.ds(pl.multiple_of(j * blk, blk), blk)],
                ring.at[slot, k], w_load.at[slot],
            ).start()

    def load_out(j, slot):
        for k in range(n_blk):
            pltpu.make_async_copy(
                w_out_hbm.at[pl.ds(pl.multiple_of(j * blk, blk), blk), pl.ds(k * blk, blk)],
                ring.at[slot, k], w_load.at[slot],
            ).start()

    def wait_slot(slot):
        pltpu.make_async_copy(ring.at[slot], ring.at[slot], w_load.at[slot]).wait()

    def fill_in(j, _):
        load_in(j, j)
        return 0

    def fill_out(j, _):
        load_out(j, n_chunks + j)
        return 0

    lax.fori_loop(0, n_chunks, fill_in, 0)
    lax.fori_loop(0, n_slots - n_chunks, fill_out, 0)

    x_cp.wait()
    g_cp.wait()
    x_f32 = x_own[...].astype(F32)
    lane = lax.broadcasted_iota(jnp.int32, (rows, 128), 1)
    sub = lax.broadcasted_iota(jnp.int32, (rows, 128), 0)
    total = jnp.sum(x_f32, axis=1, keepdims=True)
    square = jnp.sum(x_f32 * x_f32, axis=1, keepdims=True)
    packed = jnp.where(lane == sub, total, 0.0) + jnp.where(lane == sub + rows, square, 0.0)
    stats[me] = jnp.sum(packed, axis=0, keepdims=True)

    pl.semaphore_wait(barrier, N_COL * N_ROW - 1)

    def stat_copy(i):
        pc, pr = peer(i)
        return remote(stats.at[me], stats.at[me], s_send.at[i], s_recv.at[me], pc, pr)

    def x_copy(i):
        return remote(x_own, x_all.at[pl.ds(r * rows, rows)], x_send.at[i], x_recv.at[r], (c + i) % N_COL, c)

    def g_copy(i):
        return remote(gain.at[c], gain.at[c], g_send.at[i], g_recv.at[0], (c + i) % N_COL, c)

    for i in range(1, N_COL * N_ROW):
        stat_copy(i).start()
    for i in (3, 2, 1):
        x_copy(i).start()

    @pl.when(is_root)
    def _():
        for i in (3, 2, 1):
            g_copy(i).start()
        x_all[pl.ds(pl.multiple_of(r * rows, rows), rows), :] = x_own[...]

    @pl.when(jnp.logical_not(is_root))
    def _():
        x_copy(0).start()

    for i in range(1, N_COL * N_ROW):
        other = (me + i) % (N_COL * N_ROW)
        pltpu.make_async_copy(stats.at[other], stats.at[other], s_recv.at[other]).wait()

    @pl.when(jnp.logical_not(is_root))
    def _():
        pltpu.make_async_copy(gain.at[r], gain.at[r], g_recv.at[0]).wait()

    for q in range(N_ROW):
        at = pl.ds(q * rows, rows)

        @pl.when(jnp.logical_not(jnp.logical_and(is_root, r == q)))
        def _():
            pltpu.make_async_copy(x_all.at[at], x_all.at[at], x_recv.at[q]).wait()

        whole = stats[q] + stats[N_ROW + q] + stats[2 * N_ROW + q] + stats[3 * N_ROW + q]
        whole = jnp.broadcast_to(whole, (rows, 128))
        mean = jnp.sum(jnp.where(lane == sub, whole, 0.0), axis=1, keepdims=True) / d_model
        mean_sq = jnp.sum(jnp.where(lane == sub + rows, whole, 0.0), axis=1, keepdims=True) / d_model
        inv = lax.rsqrt(mean_sq - mean * mean + NORM_EPS)
        z_ref[at, :] = ((x_all[at, :].astype(F32) - mean) * inv * gain[r]).astype(BF16)

    role_near = near == c
    role_far = far == c
    role_relay = jnp.logical_not(jnp.logical_or(is_root, jnp.logical_or(role_near, role_far)))

    def near_copy(j):
        return remote(part.at[j], from_near.at[j], p_send.at[j], p_recv.at[j], c, near)

    def far_copy(j):
        return remote(part.at[j], from_far.at[j], p_send.at[j], f_recv.at[j], c, far)

    def pass_on(j):
        near_copy(j).wait_recv()
        part[j] = part[j] + from_near[j]
        far_copy(j).start()

    def up(j, _):
        wait_slot(j)
        total = jnp.dot(z_ref[:, pl.ds(0, blk)], ring[j, 0], preferred_element_type=F32)
        for k in range(1, n_blk):
            total += jnp.dot(z_ref[:, pl.ds(k * blk, blk)], ring[j, k], preferred_element_type=F32)
        part[j] = total

        @pl.when(j < 2 * n_chunks - n_slots)
        def _():
            load_out(j + n_slots - n_chunks, j)

        @pl.when(jnp.logical_or(role_near, role_relay))
        def _():
            near_copy(j).start()

        @pl.when(jnp.logical_and(role_far, j >= 1))
        def _():
            pass_on(j - 1)

        return 0

    lax.fori_loop(0, n_chunks, up, 0)

    @pl.when(role_far)
    def _():
        pass_on(n_chunks - 1)

    def up_copy(j):
        return remote(hid.at[j], hid.at[j], h_up.at[j], h_recv.at[j], (c + 1) % N_COL, r)

    def down_copy(j):
        return remote(hid.at[j], hid.at[j], h_down.at[j], h_recv.at[j], (c + N_COL - 1) % N_COL, r)

    sends_up = jnp.logical_and(c >= r, c < N_COL - 1)
    sends_down = jnp.logical_and(c <= r, c > 0)
    acc[...] = jnp.zeros_like(acc)

    def down(j, _):
        @pl.when(is_root)
        def _():
            near_copy(j).wait_recv()
            far_copy(j).wait_recv()
            hid[j] = gelu_tanh(part[j] + from_near[j] + from_far[j]).astype(BF16)

        @pl.when(jnp.logical_not(is_root))
        def _():
            up_copy(j).wait_recv()

        @pl.when(sends_up)
        def _():
            up_copy(j).start()

        @pl.when(sends_down)
        def _():
            down_copy(j).start()

        slot = (n_chunks + j) % n_slots
        wait_slot(slot)
        for k in range(n_blk):
            at = pl.ds(k * blk, blk)
            acc[:, at] += jnp.dot(hid[j], ring[slot, k], preferred_element_type=F32)
        return 0

    lax.fori_loop(0, n_chunks, down, 0)

    def near_part(i, k):
        other = near if i == 0 else (near + 2) % N_ROW
        at = pl.ds(k * blk, blk)
        return remote(
            acc.at[pl.ds(pl.multiple_of(other * rows, rows), rows), at], near_sum.at[i, :, at],
            n_send.at[i, k], n_recv.at[i, k], c, near,
        )

    def far_part(k):
        at = pl.ds(k * blk, blk)
        return remote(pair_sum.at[:, at], far_sum.at[:, at], o_send.at[k], o_recv.at[k], c, far)

    for i in (1, 0):
        for k in range(n_blk):
            near_part(i, k).start()
    for k in range(n_blk):
        at = pl.ds(k * blk, blk)
        near_part(1, k).wait_recv()
        pair_sum[:, at] = acc[pl.ds(pl.multiple_of(far * rows, rows), rows), at] + near_sum[1, :, at]
        far_part(k).start()
    for k in range(n_blk):
        at = pl.ds(k * blk, blk)
        near_part(0, k).wait_recv()
        far_part(k).wait_recv()
        own = acc[pl.ds(pl.multiple_of(r * rows, rows), rows), at] + near_sum[0, :, at] + far_sum[:, at]
        y_ref[:, at] = (x_own[:, at].astype(F32) + own).astype(BF16)

    for i in range(1, N_COL * N_ROW):
        stat_copy(i).wait_send()
    for i in (3, 2, 1):
        x_copy(i).wait_send()

    @pl.when(is_root)
    def _():
        for i in (3, 2, 1):
            g_copy(i).wait_send()

    @pl.when(jnp.logical_not(is_root))
    def _():
        x_copy(0).wait_send()

    def finish(j, _):
        @pl.when(jnp.logical_not(is_root))
        def _():
            near_copy(j).wait_send()

        @pl.when(sends_up)
        def _():
            up_copy(j).wait_send()

        @pl.when(sends_down)
        def _():
            down_copy(j).wait_send()

        return 0

    lax.fori_loop(0, n_chunks, finish, 0)
    for i in (1, 0):
        for k in range(n_blk):
            near_part(i, k).wait_send()
    for k in range(n_blk):
        far_part(k).wait_send()


def solution(mesh):
    def local_block(x_blk, gain_blk, w_in_blk, w_out_blk):
        rows, depth = x_blk.shape
        blk = depth // 4
        n_chunks = w_in_blk.shape[1] // blk
        n_slots = n_chunks + n_chunks // 2
        tokens = rows * N_ROW
        dma = pltpu.SemaphoreType.DMA
        n_all = N_COL * N_ROW
        return pl.pallas_call(
            functools.partial(mlp_kernel, n_chunks, n_slots, blk),
            out_shape=jax.ShapeDtypeStruct((rows, depth), BF16),
            in_specs=[pl.BlockSpec(memory_space=pl.ANY)] * 4,
            out_specs=pl.BlockSpec(memory_space=pltpu.VMEM),
            scratch_shapes=[
                pltpu.VMEM((rows, depth), BF16),
                pltpu.VMEM((N_COL, 1, depth), F32),
                pltpu.VMEM((n_all, 1, 128), F32),
                pltpu.VMEM((tokens, depth), BF16),
                pltpu.VMEM((tokens, depth), BF16),
                pltpu.VMEM((n_slots, depth // blk, blk, blk), BF16),
                pltpu.VMEM((n_chunks, tokens, blk), F32),
                pltpu.VMEM((n_chunks, tokens, blk), F32),
                pltpu.VMEM((n_chunks, tokens, blk), F32),
                pltpu.VMEM((n_chunks, tokens, blk), BF16),
                pltpu.VMEM((tokens, depth), F32),
                pltpu.VMEM((2, rows, depth), F32),
                pltpu.VMEM((rows, depth), F32),
                pltpu.VMEM((rows, depth), F32),
                dma((2,)), dma((n_slots,)),
                dma((N_COL,)), dma((N_ROW,)), dma((N_COL,)), dma((1,)), dma((n_all,)), dma((n_all,)),
                dma((n_chunks,)), dma((n_chunks,)), dma((n_chunks,)),
                dma((n_chunks,)), dma((n_chunks,)), dma((n_chunks,)),
                dma((2, depth // blk)), dma((2, depth // blk)), dma((depth // blk,)), dma((depth // blk,)),
            ],
            compiler_params=pltpu.CompilerParams(
                collective_id=0, has_side_effects=True, vmem_limit_bytes=67_000_000
            ),
        )(x_blk, gain_blk.reshape(1, depth), w_in_blk, w_out_blk)

    return jax.shard_map(
        local_block,
        mesh=mesh,
        in_specs=(P(("dp", "row"), "col"), P("col"), P("row", "col"), P("row", "col")),
        out_specs=P(("dp", "row"), "col"),
        check_vma=False,
    )
```

time: 179 us -> 58.6 us (0.33)
  waiting for transfers between devices: 76.7 us -> 0 us
  Pallas kernels: 0 us -> 57 us
  blocking collectives: 52.9 us -> 0 us
  matrix products: 29.3 us -> 0 us
  between operations: 13.1 us -> 0.01 us
  other arithmetic: 5.4 us -> 0 us
    pallas_call x0 -> x1, Pallas kernels: none -> 57 us  [local_block(): pl.pallas_call(functools.partial(mlp_kernel, n_chunks, n_slots, blk), out...]
    reduce_scatter x2 -> x0, waiting for transfers between devices: 48.7 us -> none  [the longest x1 28.5 us: local_block(): up_sum = lax.psum_scatter(up_part, 'row', scatter_dimension=0, tiled=True)]
    dot_general x2 -> x0, matrix products: 29.3 us -> none  [the longest x1 14.9 us: local_block(): up_part = jnp.dot(z_cols, w_in_blk, preferred_element_type=jnp.float32)]
    all_gather x1 -> x0, waiting for transfers between devices: 28 us -> none  [local_block(): h_rows = lax.all_gather(h_blk, 'col', axis=1, tiled=True)]
    all_to_all x2 -> x0, blocking collectives: 25.6 us -> none  [the longest x1 17 us: local_block(): h_cols = lax.all_to_all(h_rows, 'row', 1, 0, tiled=True)]
    all_gather x1 -> x0, blocking collectives: 13.8 us -> none  [local_block(): z_rows = lax.all_gather(z_blk, 'col', axis=1, tiled=True)]
    psum x1 -> x0, blocking collectives: 13.5 us -> none  [local_block(): row_stats = lax.psum(part_stats, 'col') / d_model]
    convert_element_type x3 -> x0, other arithmetic: 4.41 us -> none  [the longest x1 1.93 us: local_block(): h_blk = jax.nn.gelu(up_sum, approximate=True).astype(jnp.bfloat16)]
  transfers between devices with their start and end apart: 3 -> 0, of which waited for: 3 -> 0; matrix products, arithmetic and copies ran while one was open for 0% -> 0% of each run, Pallas kernels for 0% -> 0%
where the time goes in v1:
time: 58.6 us; the launch traced here: 58.5 us
  Pallas kernels  57 us (97%)
  local copies, waits for them, and re-layouts  1.47 us (3%)
    pallas_call x1, Pallas kernels, local_block(): pl.pallas_call(functools.partial(mlp_kernel, n_chunks, n_slots, blk), out...  57 us
    unnamed x1, local copies, waits for them, and re-layouts  1.47 us

profile of v1, /device:TPU:0, one launch (start us, length us, event | category | flops | bytes accessed | tf_op | source)
XLA Modules:
  0.0 58.5 jit_solution(10096235769974144979)
XLA Ops:
  0.0 57.0 %shard_map.46 = bf16[16,2048]{1,0:T(8,128)(2,1)} custom-call(bf16[16,2048]{1,0:T(8,128)(2,1)} %x_hbm.1, f32[1,2048]{1,0:T(1,128)} %bitcast.1, bf16[2048,8192]{1,0:T(8,128)(2,1)} %w_in_hbm.1, bf16[8192,2048]{1,0:T(8,128)(2,1)} %w_out_hbm.1), custom_call_target="tpu_custom_call" | custom-call | tf_op jit(solution)/shard_map/pallas_call | solution.py:296
  57.0 1.5 %copy.6 = bf16[16,2048]{1,0:T(8,128)(2,1)} copy(bf16[16,2048]{1,0:T(8,128)(2,1)} %shard_map.46) | data formatting | bytes 131072

commit v2 on v1

--- a/solution.py
+++ b/solution.py
@@ -21,9 +21,9 @@
 def mlp_kernel(
     n_chunks, n_slots, blk,
     x_hbm, g_hbm, w_in_hbm, w_out_hbm, y_ref,
-    x_own, gain, stats, x_all, z_ref, ring, part, from_near, from_far, hid, acc, near_sum, pair_sum, far_sum,
+    x_own, gain, stats, x_all, z_ref, ring, part, from_near, from_far, hid, hid_sent, acc, near_sum, pair_sum, far_sum,
     x_load, w_load, x_send, x_recv, g_send, g_recv, s_send, s_recv, p_send, p_recv, f_recv,
-    h_up, h_down, h_recv, n_send, n_recv, o_send, o_recv,
+    h_inner, h_outer, h_recv, w_send, n_send, n_recv, o_send, o_recv,
 ):
     dp, c, r = lax.axis_index("dp"), lax.axis_index("col"), lax.axis_index("row")
     rows = x_own.shape[0]
@@ -54,17 +54,15 @@
         pl.semaphore_signal(barrier, inc=1, device_id=(dp, pc, pr), device_id_type=MESH)
 
     def load_in(j, slot):
-        for k in range(n_blk):
-            pltpu.make_async_copy(
-                w_in_hbm.at[pl.ds(k * blk, blk), pl.ds(pl.multiple_of(j * blk, blk), blk)],
-                ring.at[slot, k], w_load.at[slot],
-            ).start()
+        pltpu.make_async_copy(
+            w_in_hbm.at[:, pl.ds(pl.multiple_of(j * blk, blk), blk)], ring.at[slot], w_load.at[slot]
+        ).start()
 
     def load_out(j, slot):
         for k in range(n_blk):
             pltpu.make_async_copy(
                 w_out_hbm.at[pl.ds(pl.multiple_of(j * blk, blk), blk), pl.ds(k * blk, blk)],
-                ring.at[slot, k], w_load.at[slot],
+                ring.at[slot, pl.ds(k * blk, blk)], w_load.at[slot],
             ).start()
 
     def wait_slot(slot):
@@ -79,7 +77,6 @@
         return 0
 
     lax.fori_loop(0, n_chunks, fill_in, 0)
-    lax.fori_loop(0, n_slots - n_chunks, fill_out, 0)
 
     x_cp.wait()
     g_cp.wait()
@@ -118,6 +115,8 @@
     def _():
         x_copy(0).start()
 
+    lax.fori_loop(0, n_slots - n_chunks, fill_out, 0)
+
     for i in range(1, N_COL * N_ROW):
         other = (me + i) % (N_COL * N_ROW)
         pltpu.make_async_copy(stats.at[other], stats.at[other], s_recv.at[other]).wait()
@@ -142,7 +141,19 @@
 
     role_near = near == c
     role_far = far == c
-    role_relay = jnp.logical_not(jnp.logical_or(is_root, jnp.logical_or(role_near, role_far)))
+    role_last = r == N_ROW - 1 - c
+
+    def kind_phase(j):
+        return (j + 4) % 5
+
+    def at_root(j):
+        return jnp.logical_or(kind_phase(j) == 0, kind_phase(j) == 2)
+
+    def by_root(j):
+        return jnp.logical_or(kind_phase(j) == 1, kind_phase(j) == 3)
+
+    def direct(j):
+        return kind_phase(j) == 4
 
     def near_copy(j):
         return remote(part.at[j], from_near.at[j], p_send.at[j], p_recv.at[j], c, near)
@@ -150,75 +161,141 @@
     def far_copy(j):
         return remote(part.at[j], from_far.at[j], p_send.at[j], f_recv.at[j], c, far)
 
+    def passes(j):
+        return jnp.logical_or(
+            jnp.logical_and(at_root(j), role_far), jnp.logical_and(jnp.logical_not(at_root(j)), role_near)
+        )
+
+    def ends(j):
+        return jnp.logical_or(
+            jnp.logical_and(at_root(j), is_root), jnp.logical_and(jnp.logical_not(at_root(j)), role_last)
+        )
+
+    def gives(j):
+        return jnp.logical_not(jnp.logical_or(passes(j), ends(j)))
+
     def pass_on(j):
-        near_copy(j).wait_recv()
-        part[j] = part[j] + from_near[j]
-        far_copy(j).start()
+        @pl.when(passes(j))
+        def _():
+            near_copy(j).wait_recv()
+            part[j] = part[j] + from_near[j]
+            far_copy(j).start()
 
     def up(j, _):
         wait_slot(j)
-        total = jnp.dot(z_ref[:, pl.ds(0, blk)], ring[j, 0], preferred_element_type=F32)
+        total = jnp.dot(z_ref[:, pl.ds(0, blk)], ring[j, pl.ds(0, blk)], preferred_element_type=F32)
         for k in range(1, n_blk):
-            total += jnp.dot(z_ref[:, pl.ds(k * blk, blk)], ring[j, k], preferred_element_type=F32)
+            at = pl.ds(k * blk, blk)
+            total += jnp.dot(z_ref[:, at], ring[j, at], preferred_element_type=F32)
         part[j] = total
 
         @pl.when(j < 2 * n_chunks - n_slots)
         def _():
             load_out(j + n_slots - n_chunks, j)
 
-        @pl.when(jnp.logical_or(role_near, role_relay))
+        @pl.when(gives(j))
         def _():
             near_copy(j).start()
 
-        @pl.when(jnp.logical_and(role_far, j >= 1))
+        @pl.when(j >= 1)
         def _():
             pass_on(j - 1)
 
         return 0
 
     lax.fori_loop(0, n_chunks, up, 0)
-
-    @pl.when(role_far)
-    def _():
-        pass_on(n_chunks - 1)
-
-    def up_copy(j):
-        return remote(hid.at[j], hid.at[j], h_up.at[j], h_recv.at[j], (c + 1) % N_COL, r)
-
-    def down_copy(j):
-        return remote(hid.at[j], hid.at[j], h_down.at[j], h_recv.at[j], (c + N_COL - 1) % N_COL, r)
-
-    sends_up = jnp.logical_and(c >= r, c < N_COL - 1)
-    sends_down = jnp.logical_and(c <= r, c > 0)
+    pass_on(n_chunks - 1)
+
+    inner = 1 + c % 2
+    outer = (3 * c + 2) % 5
+    inside = jnp.logical_or(c == 1, c == 2)
+    forwards = jnp.logical_or(jnp.logical_and(c == 2, r < 2), jnp.logical_and(c == 1, r >= 2))
+
+    def inner_copy(j):
+        return remote(hid.at[j], hid.at[j], h_inner.at[j], h_recv.at[j], inner, r)
+
+    def outer_copy(j):
+        return remote(hid.at[j], hid.at[j], h_outer.at[j], h_recv.at[j], outer, r)
+
+    def forward_copy(j):
+        return remote(hid.at[j], hid.at[j], h_inner.at[j], h_recv.at[j], 3 * (c - 1), r)
+
+    def last_copy(j, to):
+        return remote(hid_sent.at[j], hid.at[j], w_send.at[to, j], h_recv.at[j], to, c)
+
     acc[...] = jnp.zeros_like(acc)
-
-    def down(j, _):
-        @pl.when(is_root)
+    early_lag = jnp.where(inside | is_root, 6, 11)
+    late_lag = jnp.where(is_root, 6, early_lag + 6)
+
+    def finish_sum(j):
+        @pl.when(ends(j))
         def _():
             near_copy(j).wait_recv()
             far_copy(j).wait_recv()
-            hid[j] = gelu_tanh(part[j] + from_near[j] + from_far[j]).astype(BF16)
-
-        @pl.when(jnp.logical_not(is_root))
-        def _():
-            up_copy(j).wait_recv()
-
-        @pl.when(sends_up)
-        def _():
-            up_copy(j).start()
-
-        @pl.when(sends_down)
-        def _():
-            down_copy(j).start()
+            chunk = gelu_tanh(part[j] + from_near[j] + from_far[j]).astype(BF16)
+
+            @pl.when(is_root)
+            def _():
+                hid[j] = chunk
+                inner_copy(j).start()
+                outer_copy(j).start()
+
+            @pl.when(jnp.logical_not(is_root))
+            def _():
+                hid_sent[j] = chunk
+
+                @pl.when(by_root(j))
+                def _():
+                    last_copy(j, c).start()
+
+                @pl.when(direct(j))
+                def _():
+                    for to in range(N_COL):
+                        last_copy(j, to).start()
+
+    def use(j):
+        @pl.when(jnp.logical_not(jnp.logical_and(is_root, at_root(j))))
+        def _():
+            inner_copy(j).wait_recv()
+
+        @pl.when(jnp.logical_and(is_root, by_root(j)))
+        def _():
+            inner_copy(j).start()
+            outer_copy(j).start()
+
+        @pl.when(jnp.logical_and(forwards, jnp.logical_not(direct(j))))
+        def _():
+            forward_copy(j).start()
 
         slot = (n_chunks + j) % n_slots
         wait_slot(slot)
         for k in range(n_blk):
             at = pl.ds(k * blk, blk)
-            acc[:, at] += jnp.dot(hid[j], ring[slot, k], preferred_element_type=F32)
+            acc[:, at] += jnp.dot(hid[j], ring[slot, at], preferred_element_type=F32)
+
+    def down(t, _):
+        @pl.when(t < n_chunks)
+        def _():
+            finish_sum(t)
+
+        early = t - early_lag
+        late = t - late_lag
+
+        @pl.when(jnp.logical_and(early >= 0, early < n_chunks))
+        def _():
+            @pl.when(at_root(early))
+            def _():
+                use(early)
+
+        @pl.when(jnp.logical_and(late >= 0, late < n_chunks))
+        def _():
+            @pl.when(jnp.logical_not(at_root(late)))
+            def _():
+                use(late)
+
         return 0
 
-    lax.fori_loop(0, n_chunks, down, 0)
+    lax.fori_loop(0, n_chunks + 17, down, 0)
 
     def near_part(i, k):
         other = near if i == 0 else (near + 2) % N_ROW
@@ -262,17 +339,27 @@
         x_copy(0).wait_send()
 
     def finish(j, _):
-        @pl.when(jnp.logical_not(is_root))
+        @pl.when(jnp.logical_not(ends(j)))
         def _():
             near_copy(j).wait_send()
 
-        @pl.when(sends_up)
-        def _():
-            up_copy(j).wait_send()
-
-        @pl.when(sends_down)
-        def _():
-            down_copy(j).wait_send()
+        @pl.when(jnp.logical_and(is_root, jnp.logical_not(direct(j))))
+        def _():
+            inner_copy(j).wait_send()
+            outer_copy(j).wait_send()
+
+        @pl.when(jnp.logical_and(forwards, jnp.logical_not(direct(j))))
+        def _():
+            forward_copy(j).wait_send()
+
+        @pl.when(jnp.logical_and(role_last, by_root(j)))
+        def _():
+            last_copy(j, c).wait_send()
+
+        @pl.when(jnp.logical_and(role_last, direct(j)))
+        def _():
+            for to in range(N_COL):
+                last_copy(j, to).wait_send()
 
         return 0
 
@@ -287,7 +374,7 @@
 def solution(mesh):
     def local_block(x_blk, gain_blk, w_in_blk, w_out_blk):
         rows, depth = x_blk.shape
-        blk = depth // 4
+        blk = depth // 8
         n_chunks = w_in_blk.shape[1] // blk
         n_slots = n_chunks + n_chunks // 2
         tokens = rows * N_ROW
@@ -304,10 +391,11 @@
                 pltpu.VMEM((n_all, 1, 128), F32),
                 pltpu.VMEM((tokens, depth), BF16),
                 pltpu.VMEM((tokens, depth), BF16),
-                pltpu.VMEM((n_slots, depth // blk, blk, blk), BF16),
+                pltpu.VMEM((n_slots, depth, blk), BF16),
                 pltpu.VMEM((n_chunks, tokens, blk), F32),
                 pltpu.VMEM((n_chunks, tokens, blk), F32),
                 pltpu.VMEM((n_chunks, tokens, blk), F32),
+                pltpu.VMEM((n_chunks, tokens, blk), BF16),
                 pltpu.VMEM((n_chunks, tokens, blk), BF16),
                 pltpu.VMEM((tokens, depth), F32),
                 pltpu.VMEM((2, rows, depth), F32),
@@ -316,7 +404,7 @@
                 dma((2,)), dma((n_slots,)),
                 dma((N_COL,)), dma((N_ROW,)), dma((N_COL,)), dma((1,)), dma((n_all,)), dma((n_all,)),
                 dma((n_chunks,)), dma((n_chunks,)), dma((n_chunks,)),
-                dma((n_chunks,)), dma((n_chunks,)), dma((n_chunks,)),
+                dma((n_chunks,)), dma((n_chunks,)), dma((n_chunks,)), dma((N_COL, n_chunks)),
                 dma((2, depth // blk)), dma((2, depth // blk)), dma((depth // blk,)), dma((depth // blk,)),
             ],
             compiler_params=pltpu.CompilerParams(

time: 58.6 us -> 63.8 us (1.089)
  Pallas kernels: 57 us -> 62.2 us
    pallas_call x1, Pallas kernels: 57 us -> 62.2 us  [local_block(): pl.pallas_call(functools.partial(mlp_kernel, n_chunks, n_slots, blk), out...]
where the time goes in v2:
time: 63.8 us; the launch traced here: 63.7 us
  Pallas kernels  62.2 us (97%)
  local copies, waits for them, and re-layouts  1.47 us (2%)
    pallas_call x1, Pallas kernels, local_block(): pl.pallas_call(functools.partial(mlp_kernel, n_chunks, n_slots, blk), out...  62.2 us
    unnamed x1, local copies, waits for them, and re-layouts  1.47 us

profile of v2, /device:TPU:0, one launch (start us, length us, event | category | flops | bytes accessed | tf_op | source)
XLA Modules:
  0.0 63.7 jit_solution(7875344338353132494)
XLA Ops:
  0.0 62.2 %shard_map.46 = bf16[16,2048]{1,0:T(8,128)(2,1)} custom-call(bf16[16,2048]{1,0:T(8,128)(2,1)} %x_hbm.1, f32[1,2048]{1,0:T(1,128)} %bitcast.1, bf16[2048,8192]{1,0:T(8,128)(2,1)} %w_in_hbm.1, bf16[8192,2048]{1,0:T(8,128)(2,1)} %w_out_hbm.1), custom_call_target="tpu_custom_call" | custom-call | tf_op jit(solution)/shard_map/pallas_call | solution.py:383
  62.2 1.5 %copy.6 = bf16[16,2048]{1,0:T(8,128)(2,1)} copy(bf16[16,2048]{1,0:T(8,128)(2,1)} %shard_map.46) | data formatting | bytes 131072

commit v3 on v2

--- a/solution.py
+++ b/solution.py
@@ -224,8 +224,8 @@
         return remote(hid_sent.at[j], hid.at[j], w_send.at[to, j], h_recv.at[j], to, c)
 
     acc[...] = jnp.zeros_like(acc)
-    early_lag = jnp.where(inside | is_root, 6, 11)
-    late_lag = jnp.where(is_root, 6, early_lag + 6)
+    early_lag = jnp.where(inside | is_root, 3, 6)
+    late_lag = jnp.where(is_root, 3, early_lag + 3)
 
     def finish_sum(j):
         @pl.when(ends(j))
@@ -295,7 +295,7 @@
 
         return 0
 
-    lax.fori_loop(0, n_chunks + 17, down, 0)
+    lax.fori_loop(0, n_chunks + 9, down, 0)
 
     def near_part(i, k):
         other = near if i == 0 else (near + 2) % N_ROW
@@ -374,7 +374,7 @@
 def solution(mesh):
     def local_block(x_blk, gain_blk, w_in_blk, w_out_blk):
         rows, depth = x_blk.shape
-        blk = depth // 8
+        blk = depth // 4
         n_chunks = w_in_blk.shape[1] // blk
         n_slots = n_chunks + n_chunks // 2
         tokens = rows * N_ROW

time: 63.8 us -> 60.4 us (0.947)
  Pallas kernels: 62.2 us -> 58.7 us
    pallas_call x1, Pallas kernels: 62.2 us -> 58.7 us  [local_block(): pl.pallas_call(functools.partial(mlp_kernel, n_chunks, n_slots, blk), out...]
where the time goes in v3:
time: 60.4 us; the launch traced here: 60.2 us
  Pallas kernels  58.7 us (97%)
  local copies, waits for them, and re-layouts  1.47 us (2%)
    pallas_call x1, Pallas kernels, local_block(): pl.pallas_call(functools.partial(mlp_kernel, n_chunks, n_slots, blk), out...  58.7 us
    unnamed x1, local copies, waits for them, and re-layouts  1.47 us

profile of v3, /device:TPU:0, one launch (start us, length us, event | category | flops | bytes accessed | tf_op | source)
XLA Modules:
  0.0 60.2 jit_solution(11375279700408701850)
XLA Ops:
  0.0 58.7 %shard_map.46 = bf16[16,2048]{1,0:T(8,128)(2,1)} custom-call(bf16[16,2048]{1,0:T(8,128)(2,1)} %x_hbm.1, f32[1,2048]{1,0:T(1,128)} %bitcast.1, bf16[2048,8192]{1,0:T(8,128)(2,1)} %w_in_hbm.1, bf16[8192,2048]{1,0:T(8,128)(2,1)} %w_out_hbm.1), custom_call_target="tpu_custom_call" | custom-call | tf_op jit(solution)/shard_map/pallas_call | solution.py:383
  58.7 1.5 %copy.6 = bf16[16,2048]{1,0:T(8,128)(2,1)} copy(bf16[16,2048]{1,0:T(8,128)(2,1)} %shard_map.46) | data formatting | bytes 131072

commit v4 on v3

--- a/solution.py
+++ b/solution.py
@@ -181,7 +181,7 @@
             part[j] = part[j] + from_near[j]
             far_copy(j).start()
 
-    def up(j, _):
+    def up(j):
         wait_slot(j)
         total = jnp.dot(z_ref[:, pl.ds(0, blk)], ring[j, pl.ds(0, blk)], preferred_element_type=F32)
         for k in range(1, n_blk):
@@ -197,14 +197,6 @@
         def _():
             near_copy(j).start()
 
-        @pl.when(j >= 1)
-        def _():
-            pass_on(j - 1)
-
-        return 0
-
-    lax.fori_loop(0, n_chunks, up, 0)
-    pass_on(n_chunks - 1)
 
     inner = 1 + c % 2
     outer = (3 * c + 2) % 5
@@ -224,8 +216,10 @@
         return remote(hid_sent.at[j], hid.at[j], w_send.at[to, j], h_recv.at[j], to, c)
 
     acc[...] = jnp.zeros_like(acc)
-    early_lag = jnp.where(inside | is_root, 3, 6)
-    late_lag = jnp.where(is_root, 3, early_lag + 3)
+    sum_lag = (5 * n_chunks) // 8
+    behind = 5
+    early_lag = jnp.where(is_root, sum_lag + 2, jnp.where(role_last & jnp.logical_not(inside), n_chunks + behind, n_chunks))
+    late_lag = jnp.where(is_root, sum_lag + behind, early_lag + behind)
 
     def finish_sum(j):
         @pl.when(ends(j))
@@ -273,10 +267,18 @@
             at = pl.ds(k * blk, blk)
             acc[:, at] += jnp.dot(hid[j], ring[slot, at], preferred_element_type=F32)
 
-    def down(t, _):
+    def step(t, _):
         @pl.when(t < n_chunks)
         def _():
-            finish_sum(t)
+            up(t)
+
+        @pl.when(jnp.logical_and(t >= 1, t <= n_chunks))
+        def _():
+            pass_on(t - 1)
+
+        @pl.when(jnp.logical_and(t >= sum_lag, t < n_chunks + sum_lag))
+        def _():
+            finish_sum(t - sum_lag)
 
         early = t - early_lag
         late = t - late_lag
@@ -295,7 +297,7 @@
 
         return 0
 
-    lax.fori_loop(0, n_chunks + 9, down, 0)
+    lax.fori_loop(0, 2 * n_chunks + 2 * behind, step, 0)
 
     def near_part(i, k):
         other = near if i == 0 else (near + 2) % N_ROW
@@ -317,6 +319,47 @@
         near_part(1, k).wait_recv()
         pair_sum[:, at] = acc[pl.ds(pl.multiple_of(far * rows, rows), rows), at] + near_sum[1, :, at]
         far_part(k).start()
+    for i in range(1, N_COL * N_ROW):
+        stat_copy(i).wait_send()
+    for i in (3, 2, 1):
+        x_copy(i).wait_send()
+
+    @pl.when(is_root)
+    def _():
+        for i in (3, 2, 1):
+            g_copy(i).wait_send()
+
+    @pl.when(jnp.logical_not(is_root))
+    def _():
+        x_copy(0).wait_send()
+
+    def finish(j, _):
+        @pl.when(jnp.logical_not(ends(j)))
+        def _():
+            near_copy(j).wait_send()
+
+        @pl.when(jnp.logical_and(is_root, jnp.logical_not(direct(j))))
+        def _():
+            inner_copy(j).wait_send()
+            outer_copy(j).wait_send()
+
+        @pl.when(jnp.logical_and(forwards, jnp.logical_not(direct(j))))
+        def _():
+            forward_copy(j).wait_send()
+
+        @pl.when(jnp.logical_and(role_last, by_root(j)))
+        def _():
+            last_copy(j, c).wait_send()
+
+        @pl.when(jnp.logical_and(role_last, direct(j)))
+        def _():
+            for to in range(N_COL):
+                last_copy(j, to).wait_send()
+
+        return 0
+
+    lax.fori_loop(0, n_chunks, finish, 0)
+
     for k in range(n_blk):
         at = pl.ds(k * blk, blk)
         near_part(0, k).wait_recv()
@@ -324,46 +367,6 @@
         own = acc[pl.ds(pl.multiple_of(r * rows, rows), rows), at] + near_sum[0, :, at] + far_sum[:, at]
         y_ref[:, at] = (x_own[:, at].astype(F32) + own).astype(BF16)
 
-    for i in range(1, N_COL * N_ROW):
-        stat_copy(i).wait_send()
-    for i in (3, 2, 1):
-        x_copy(i).wait_send()
-
-    @pl.when(is_root)
-    def _():
-        for i in (3, 2, 1):
-            g_copy(i).wait_send()
-
-    @pl.when(jnp.logical_not(is_root))
-    def _():
-        x_copy(0).wait_send()
-
-    def finish(j, _):
-        @pl.when(jnp.logical_not(ends(j)))
-        def _():
-            near_copy(j).wait_send()
-
-        @pl.when(jnp.logical_and(is_root, jnp.logical_not(direct(j))))
-        def _():
-            inner_copy(j).wait_send()
-            outer_copy(j).wait_send()
-
-        @pl.when(jnp.logical_and(forwards, jnp.logical_not(direct(j))))
-        def _():
-            forward_copy(j).wait_send()
-
-        @pl.when(jnp.logical_and(role_last, by_root(j)))
-        def _():
-            last_copy(j, c).wait_send()
-
-        @pl.when(jnp.logical_and(role_last, direct(j)))
-        def _():
-            for to in range(N_COL):
-                last_copy(j, to).wait_send()
-
-        return 0
-
-    lax.fori_loop(0, n_chunks, finish, 0)
     for i in (1, 0):
         for k in range(n_blk):
             near_part(i, k).wait_send()

time: 60.4 us -> 58 us (0.960)
  Pallas kernels: 58.7 us -> 56.3 us
    pallas_call x1, Pallas kernels: 58.7 us -> 56.3 us  [local_block(): pl.pallas_call(functools.partial(mlp_kernel, n_chunks, n_slots, blk), out...]
where the time goes in v4:
time: 58 us; the launch traced here: 57.8 us
  Pallas kernels  56.3 us (97%)
  local copies, waits for them, and re-layouts  1.47 us (3%)
    pallas_call x1, Pallas kernels, local_block(): pl.pallas_call(functools.partial(mlp_kernel, n_chunks, n_slots, blk), out...  56.3 us
    unnamed x1, local copies, waits for them, and re-layouts  1.47 us

profile of v4, /device:TPU:0, one launch (start us, length us, event | category | flops | bytes accessed | tf_op | source)
XLA Modules:
  0.0 57.8 jit_solution(5093187792150858661)
XLA Ops:
  0.0 56.3 %shard_map.46 = bf16[16,2048]{1,0:T(8,128)(2,1)} custom-call(bf16[16,2048]{1,0:T(8,128)(2,1)} %x_hbm.1, f32[1,2048]{1,0:T(1,128)} %bitcast.1, bf16[2048,8192]{1,0:T(8,128)(2,1)} %w_in_hbm.1, bf16[8192,2048]{1,0:T(8,128)(2,1)} %w_out_hbm.1), custom_call_target="tpu_custom_call" | custom-call | tf_op jit(solution)/shard_map/pallas_call | solution.py:386
  56.4 1.5 %copy.6 = bf16[16,2048]{1,0:T(8,128)(2,1)} copy(bf16[16,2048]{1,0:T(8,128)(2,1)} %shard_map.46) | data formatting | bytes 131072

commit v5 on v4

--- a/solution.py
+++ b/solution.py
@@ -12,6 +12,7 @@
 BF16, F32 = jnp.bfloat16, jnp.float32
 N_COL = 4
 N_ROW = 4
+KINDS = (0, 1, 0, 1, 0, 2, 0, 1, 0, 2, 0, 1, 0, 2, 2, 2)
 
 
 def gelu_tanh(x):
@@ -20,10 +21,10 @@
 
 def mlp_kernel(
     n_chunks, n_slots, blk,
-    x_hbm, g_hbm, w_in_hbm, w_out_hbm, y_ref,
-    x_own, gain, stats, x_all, z_ref, ring, part, from_near, from_far, hid, hid_sent, acc, near_sum, pair_sum, far_sum,
+    x_hbm, g_hbm, w_in_hbm, w_out_hbm, y_hbm,
+    x_own, gain, stats, x_all, z_ref, ring, part, from_near, from_far, hid, hid_sent, acc, near_sum, pair_sum, far_sum, y_ref,
     x_load, w_load, x_send, x_recv, g_send, g_recv, s_send, s_recv, p_send, p_recv, f_recv,
-    h_inner, h_outer, h_recv, w_send, n_send, n_recv, o_send, o_recv,
+    h_inner, h_outer, h_recv, w_send, n_send, n_recv, o_send, o_recv, y_store,
 ):
     dp, c, r = lax.axis_index("dp"), lax.axis_index("col"), lax.axis_index("row")
     rows = x_own.shape[0]
@@ -94,11 +95,20 @@
         pc, pr = peer(i)
         return remote(stats.at[me], stats.at[me], s_send.at[i], s_recv.at[me], pc, pr)
 
+    def far_first(i):
+        if i == 0:
+            return c
+        if i == 3:
+            return jnp.where(c < 2, 3, 0)
+        if i == 2:
+            return jnp.where(c < 2, 2, 1)
+        return jnp.where(c < 2, 1 - c, 5 - c)
+
     def x_copy(i):
-        return remote(x_own, x_all.at[pl.ds(r * rows, rows)], x_send.at[i], x_recv.at[r], (c + i) % N_COL, c)
+        return remote(x_own, x_all.at[pl.ds(r * rows, rows)], x_send.at[i], x_recv.at[r], far_first(i), c)
 
     def g_copy(i):
-        return remote(gain.at[c], gain.at[c], g_send.at[i], g_recv.at[0], (c + i) % N_COL, c)
+        return remote(gain.at[c], gain.at[c], g_send.at[i], g_recv.at[0], far_first(i), c)
 
     for i in range(1, N_COL * N_ROW):
         stat_copy(i).start()
@@ -143,17 +153,18 @@
     role_far = far == c
     role_last = r == N_ROW - 1 - c
 
-    def kind_phase(j):
-        return (j + 4) % 5
+    def one_of(j, kind):
+        found = [j == i for i in range(n_chunks) if KINDS[i % len(KINDS)] == kind]
+        return functools.reduce(jnp.logical_or, found)
 
     def at_root(j):
-        return jnp.logical_or(kind_phase(j) == 0, kind_phase(j) == 2)
+        return one_of(j, 0)
 
     def by_root(j):
-        return jnp.logical_or(kind_phase(j) == 1, kind_phase(j) == 3)
+        return one_of(j, 1)
 
     def direct(j):
-        return kind_phase(j) == 4
+        return one_of(j, 2)
 
     def near_copy(j):
         return remote(part.at[j], from_near.at[j], p_send.at[j], p_recv.at[j], c, near)
@@ -181,22 +192,40 @@
             part[j] = part[j] + from_near[j]
             far_copy(j).start()
 
-    def up(j):
-        wait_slot(j)
+    def product(j):
         total = jnp.dot(z_ref[:, pl.ds(0, blk)], ring[j, pl.ds(0, blk)], preferred_element_type=F32)
         for k in range(1, n_blk):
             at = pl.ds(k * blk, blk)
             total += jnp.dot(z_ref[:, at], ring[j, at], preferred_element_type=F32)
-        part[j] = total
-
-        @pl.when(j < 2 * n_chunks - n_slots)
-        def _():
-            load_out(j + n_slots - n_chunks, j)
-
-        @pl.when(gives(j))
-        def _():
-            near_copy(j).start()
-
+        return total
+
+    def up(i, _):
+        pair = (2 * i, 2 * i + 1)
+        for j in pair:
+            wait_slot(j)
+        totals = [product(j) for j in pair]
+        for j, total in zip(pair, totals):
+            part[j] = total
+        for j in pair:
+            @pl.when(gives(j))
+            def _():
+                near_copy(j).start()
+
+        @pl.when(i < (2 * n_chunks - n_slots) // 2)
+        def _():
+            for j in pair:
+                load_out(j + n_slots - n_chunks, j)
+
+        @pl.when(i >= 1)
+        def _():
+            for j in pair:
+                pass_on(j - 2)
+
+        return 0
+
+    lax.fori_loop(0, n_chunks // 2, up, 0)
+    for j in (n_chunks - 2, n_chunks - 1):
+        pass_on(j)
 
     inner = 1 + c % 2
     outer = (3 * c + 2) % 5
@@ -216,10 +245,10 @@
         return remote(hid_sent.at[j], hid.at[j], w_send.at[to, j], h_recv.at[j], to, c)
 
     acc[...] = jnp.zeros_like(acc)
-    sum_lag = (5 * n_chunks) // 8
-    behind = 5
-    early_lag = jnp.where(is_root, sum_lag + 2, jnp.where(role_last & jnp.logical_not(inside), n_chunks + behind, n_chunks))
-    late_lag = jnp.where(is_root, sum_lag + behind, early_lag + behind)
+    behind = 3
+    lag = jnp.where(is_root, 1, jnp.where(role_last, jnp.where(inside, n_chunks // 2, n_chunks), 0))
+    root_lag = jnp.where(is_root, behind, lag + behind)
+    direct_lag = jnp.where(is_root, n_chunks // 2, lag + behind)
 
     def finish_sum(j):
         @pl.when(ends(j))
@@ -267,37 +296,24 @@
             at = pl.ds(k * blk, blk)
             acc[:, at] += jnp.dot(hid[j], ring[slot, at], preferred_element_type=F32)
 
+    def take(j, wanted):
+        @pl.when(jnp.logical_and(j >= 0, j < n_chunks))
+        def _():
+            @pl.when(wanted(j))
+            def _():
+                use(j)
+
     def step(t, _):
         @pl.when(t < n_chunks)
         def _():
-            up(t)
-
-        @pl.when(jnp.logical_and(t >= 1, t <= n_chunks))
-        def _():
-            pass_on(t - 1)
-
-        @pl.when(jnp.logical_and(t >= sum_lag, t < n_chunks + sum_lag))
-        def _():
-            finish_sum(t - sum_lag)
-
-        early = t - early_lag
-        late = t - late_lag
-
-        @pl.when(jnp.logical_and(early >= 0, early < n_chunks))
-        def _():
-            @pl.when(at_root(early))
-            def _():
-                use(early)
-
-        @pl.when(jnp.logical_and(late >= 0, late < n_chunks))
-        def _():
-            @pl.when(jnp.logical_not(at_root(late)))
-            def _():
-                use(late)
-
+            finish_sum(t)
+
+        take(t - lag, at_root)
+        take(t - direct_lag, direct)
+        take(t - root_lag, by_root)
         return 0
 
-    lax.fori_loop(0, 2 * n_chunks + 2 * behind, step, 0)
+    lax.fori_loop(0, 2 * n_chunks + behind, step, 0)
 
     def near_part(i, k):
         other = near if i == 0 else (near + 2) % N_ROW
@@ -310,6 +326,10 @@
     def far_part(k):
         at = pl.ds(k * blk, blk)
         return remote(pair_sum.at[:, at], far_sum.at[:, at], o_send.at[k], o_recv.at[k], c, far)
+
+    def store(k):
+        at = pl.ds(k * blk, blk)
+        return pltpu.make_async_copy(y_ref.at[:, at], y_hbm.at[:, at], y_store.at[k])
 
     for i in (1, 0):
         for k in range(n_blk):
@@ -366,12 +386,14 @@
         far_part(k).wait_recv()
         own = acc[pl.ds(pl.multiple_of(r * rows, rows), rows), at] + near_sum[0, :, at] + far_sum[:, at]
         y_ref[:, at] = (x_own[:, at].astype(F32) + own).astype(BF16)
+        store(k).start()
 
     for i in (1, 0):
         for k in range(n_blk):
             near_part(i, k).wait_send()
     for k in range(n_blk):
         far_part(k).wait_send()
+        store(k).wait()
 
 
 def solution(mesh):
@@ -387,7 +409,7 @@
             functools.partial(mlp_kernel, n_chunks, n_slots, blk),
             out_shape=jax.ShapeDtypeStruct((rows, depth), BF16),
             in_specs=[pl.BlockSpec(memory_space=pl.ANY)] * 4,
-            out_specs=pl.BlockSpec(memory_space=pltpu.VMEM),
+            out_specs=pl.BlockSpec(memory_space=pl.ANY),
             scratch_shapes=[
                 pltpu.VMEM((rows, depth), BF16),
                 pltpu.VMEM((N_COL, 1, depth), F32),
@@ -404,11 +426,12 @@
                 pltpu.VMEM((2, rows, depth), F32),
                 pltpu.VMEM((rows, depth), F32),
                 pltpu.VMEM((rows, depth), F32),
+                pltpu.VMEM((rows, depth), BF16),
                 dma((2,)), dma((n_slots,)),
                 dma((N_COL,)), dma((N_ROW,)), dma((N_COL,)), dma((1,)), dma((n_all,)), dma((n_all,)),
                 dma((n_chunks,)), dma((n_chunks,)), dma((n_chunks,)),
                 dma((n_chunks,)), dma((n_chunks,)), dma((n_chunks,)), dma((N_COL, n_chunks)),
-                dma((2, depth // blk)), dma((2, depth // blk)), dma((depth // blk,)), dma((depth // blk,)),
+                dma((2, depth // blk)), dma((2, depth // blk)), dma((depth // blk,)), dma((depth // blk,)), dma((depth // blk,)),
             ],
             compiler_params=pltpu.CompilerParams(
                 collective_id=0, has_side_effects=True, vmem_limit_bytes=67_000_000

time: 58 us -> 57.7 us (level)
  no operation moved by 1% of the time
where the time goes in v5:
time: 57.7 us; the launch traced here: 57.6 us
  Pallas kernels  56.1 us (97%)
  local copies, waits for them, and re-layouts  1.47 us (3%)
    pallas_call x1, Pallas kernels, local_block(): pl.pallas_call(functools.partial(mlp_kernel, n_chunks, n_slots, blk), out...  56.1 us
    unnamed x1, local copies, waits for them, and re-layouts  1.47 us

profile of v5, /device:TPU:0, one launch (start us, length us, event | category | flops | bytes accessed | tf_op | source)
XLA Modules:
  0.0 57.6 jit_solution(589904437504915324)
XLA Ops:
  0.0 56.1 %shard_map.46 = bf16[16,2048]{1,0:T(8,128)(2,1)} custom-call(bf16[16,2048]{1,0:T(8,128)(2,1)} %x_hbm.1, f32[1,2048]{1,0:T(1,128)} %bitcast.1, bf16[2048,8192]{1,0:T(8,128)(2,1)} %w_in_hbm.1, bf16[8192,2048]{1,0:T(8,128)(2,1)} %w_out_hbm.1), custom_call_target="tpu_custom_call" | custom-call | tf_op jit(solution)/shard_map/pallas_call | solution.py:408
  56.1 1.5 %copy.6 = bf16[16,2048]{1,0:T(8,128)(2,1)} copy(bf16[16,2048]{1,0:T(8,128)(2,1)} %shard_map.46) | data formatting | bytes 131072

commit v6 on v5

--- a/solution.py
+++ b/solution.py
@@ -24,7 +24,7 @@
     x_hbm, g_hbm, w_in_hbm, w_out_hbm, y_hbm,
     x_own, gain, stats, x_all, z_ref, ring, part, from_near, from_far, hid, hid_sent, acc, near_sum, pair_sum, far_sum, y_ref,
     x_load, w_load, x_send, x_recv, g_send, g_recv, s_send, s_recv, p_send, p_recv, f_recv,
-    h_inner, h_outer, h_recv, w_send, n_send, n_recv, o_send, o_recv, y_store,
+    h_send, h_recv, w_send, n_send, n_recv, o_send, o_recv, y_store,
 ):
     dp, c, r = lax.axis_index("dp"), lax.axis_index("col"), lax.axis_index("row")
     rows = x_own.shape[0]
@@ -56,18 +56,20 @@
 
     def load_in(j, slot):
         pltpu.make_async_copy(
-            w_in_hbm.at[:, pl.ds(pl.multiple_of(j * blk, blk), blk)], ring.at[slot], w_load.at[slot]
+            w_in_hbm.at[:, pl.ds(pl.multiple_of(j * blk, blk), blk)], ring.at[slot], w_load.at[j // 4]
         ).start()
 
     def load_out(j, slot):
         for k in range(n_blk):
             pltpu.make_async_copy(
                 w_out_hbm.at[pl.ds(pl.multiple_of(j * blk, blk), blk), pl.ds(k * blk, blk)],
-                ring.at[slot, pl.ds(k * blk, blk)], w_load.at[slot],
+                ring.at[slot, pl.ds(k * blk, blk)], w_load.at[n_chunks // 4 + j // n_half],
             ).start()
 
-    def wait_slot(slot):
-        pltpu.make_async_copy(ring.at[slot], ring.at[slot], w_load.at[slot]).wait()
+    n_half = n_chunks // 2
+
+    def done(ref, sem):
+        pltpu.make_async_copy(ref, ref, sem).wait()
 
     def fill_in(j, _):
         load_in(j, j)
@@ -93,7 +95,7 @@
 
     def stat_copy(i):
         pc, pr = peer(i)
-        return remote(stats.at[me], stats.at[me], s_send.at[i], s_recv.at[me], pc, pr)
+        return remote(stats.at[me], stats.at[me], s_send.at[0], s_recv.at[0], pc, pr)
 
     def far_first(i):
         if i == 0:
@@ -105,10 +107,15 @@
         return jnp.where(c < 2, 1 - c, 5 - c)
 
     def x_copy(i):
-        return remote(x_own, x_all.at[pl.ds(r * rows, rows)], x_send.at[i], x_recv.at[r], far_first(i), c)
+        return remote(x_own, x_all.at[pl.ds(r * rows, rows)], x_send.at[0], x_recv.at[0], far_first(i), c)
 
     def g_copy(i):
-        return remote(gain.at[c], gain.at[c], g_send.at[i], g_recv.at[0], far_first(i), c)
+        return remote(gain.at[c], gain.at[c], g_send.at[0], g_recv.at[0], far_first(i), c)
+
+    @pl.when(is_root)
+    def _():
+        for i in (3, 2, 1):
+            g_copy(i).start()
 
     for i in range(1, N_COL * N_ROW):
         stat_copy(i).start()
@@ -117,8 +124,6 @@
 
     @pl.when(is_root)
     def _():
-        for i in (3, 2, 1):
-            g_copy(i).start()
         x_all[pl.ds(pl.multiple_of(r * rows, rows), rows), :] = x_own[...]
 
     @pl.when(jnp.logical_not(is_root))
@@ -127,21 +132,19 @@
 
     lax.fori_loop(0, n_slots - n_chunks, fill_out, 0)
 
-    for i in range(1, N_COL * N_ROW):
-        other = (me + i) % (N_COL * N_ROW)
-        pltpu.make_async_copy(stats.at[other], stats.at[other], s_recv.at[other]).wait()
+    done(stats.at[pl.ds(0, N_COL * N_ROW - 1)], s_recv.at[0])
+
+    @pl.when(is_root)
+    def _():
+        done(x_all.at[pl.ds(0, (N_ROW - 1) * rows)], x_recv.at[0])
 
     @pl.when(jnp.logical_not(is_root))
     def _():
-        pltpu.make_async_copy(gain.at[r], gain.at[r], g_recv.at[0]).wait()
+        done(gain.at[0], g_recv.at[0])
+        done(x_all, x_recv.at[0])
 
     for q in range(N_ROW):
         at = pl.ds(q * rows, rows)
-
-        @pl.when(jnp.logical_not(jnp.logical_and(is_root, r == q)))
-        def _():
-            pltpu.make_async_copy(x_all.at[at], x_all.at[at], x_recv.at[q]).wait()
-
         whole = stats[q] + stats[N_ROW + q] + stats[2 * N_ROW + q] + stats[3 * N_ROW + q]
         whole = jnp.broadcast_to(whole, (rows, 128))
         mean = jnp.sum(jnp.where(lane == sub, whole, 0.0), axis=1, keepdims=True) / d_model
@@ -167,10 +170,10 @@
         return one_of(j, 2)
 
     def near_copy(j):
-        return remote(part.at[j], from_near.at[j], p_send.at[j], p_recv.at[j], c, near)
+        return remote(part.at[j], from_near.at[j], p_send.at[0], p_recv.at[j], c, near)
 
     def far_copy(j):
-        return remote(part.at[j], from_far.at[j], p_send.at[j], f_recv.at[j], c, far)
+        return remote(part.at[j], from_far.at[j], p_send.at[0], f_recv.at[j], c, far)
 
     def passes(j):
         return jnp.logical_or(
@@ -201,8 +204,11 @@
 
     def up(i, _):
         pair = (2 * i, 2 * i + 1)
-        for j in pair:
-            wait_slot(j)
+
+        @pl.when(i % 2 == 0)
+        def _():
+            done(ring.at[pl.ds(0, 4)], w_load.at[i // 2])
+
         totals = [product(j) for j in pair]
         for j, total in zip(pair, totals):
             part[j] = total
@@ -233,22 +239,24 @@
     forwards = jnp.logical_or(jnp.logical_and(c == 2, r < 2), jnp.logical_and(c == 1, r >= 2))
 
     def inner_copy(j):
-        return remote(hid.at[j], hid.at[j], h_inner.at[j], h_recv.at[j], inner, r)
+        return remote(hid.at[j], hid.at[j], h_send.at[0], h_recv.at[j], inner, r)
 
     def outer_copy(j):
-        return remote(hid.at[j], hid.at[j], h_outer.at[j], h_recv.at[j], outer, r)
+        return remote(hid.at[j], hid.at[j], h_send.at[0], h_recv.at[j], outer, r)
 
     def forward_copy(j):
-        return remote(hid.at[j], hid.at[j], h_inner.at[j], h_recv.at[j], 3 * (c - 1), r)
+        return remote(hid.at[j], hid.at[j], h_send.at[0], h_recv.at[j], 3 * (c - 1), r)
 
     def last_copy(j, to):
-        return remote(hid_sent.at[j], hid.at[j], w_send.at[to, j], h_recv.at[j], to, c)
+        return remote(hid_sent.at[j], hid.at[j], w_send.at[0], h_recv.at[j], to, c)
 
     acc[...] = jnp.zeros_like(acc)
     behind = 3
     lag = jnp.where(is_root, 1, jnp.where(role_last, jnp.where(inside, n_chunks // 2, n_chunks), 0))
     root_lag = jnp.where(is_root, behind, lag + behind)
-    direct_lag = jnp.where(is_root, n_chunks // 2, lag + behind)
+    direct_lag = jnp.where(is_root, 4, lag - 4)
+    second_half = jnp.where(is_root, lag, direct_lag) + n_half
+    done(ring.at[pl.ds(n_chunks, n_half)], w_load.at[n_chunks // 4])
 
     def finish_sum(j):
         @pl.when(ends(j))
@@ -291,7 +299,6 @@
             forward_copy(j).start()
 
         slot = (n_chunks + j) % n_slots
-        wait_slot(slot)
         for k in range(n_blk):
             at = pl.ds(k * blk, blk)
             acc[:, at] += jnp.dot(hid[j], ring[slot, at], preferred_element_type=F32)
@@ -307,6 +314,10 @@
         @pl.when(t < n_chunks)
         def _():
             finish_sum(t)
+
+        @pl.when(t == second_half)
+        def _():
+            done(ring.at[pl.ds(0, n_half)], w_load.at[n_chunks // 4 + 1])
 
         take(t - lag, at_root)
         take(t - direct_lag, direct)
@@ -320,16 +331,16 @@
         at = pl.ds(k * blk, blk)
         return remote(
             acc.at[pl.ds(pl.multiple_of(other * rows, rows), rows), at], near_sum.at[i, :, at],
-            n_send.at[i, k], n_recv.at[i, k], c, near,
+            n_send.at[0], n_recv.at[i, k], c, near,
         )
 
     def far_part(k):
         at = pl.ds(k * blk, blk)
-        return remote(pair_sum.at[:, at], far_sum.at[:, at], o_send.at[k], o_recv.at[k], c, far)
+        return remote(pair_sum.at[:, at], far_sum.at[:, at], o_send.at[0], o_recv.at[k], c, far)
 
     def store(k):
         at = pl.ds(k * blk, blk)
-        return pltpu.make_async_copy(y_ref.at[:, at], y_hbm.at[:, at], y_store.at[k])
+        return pltpu.make_async_copy(y_ref.at[:, at], y_hbm.at[:, at], y_store.at[0])
 
     for i in (1, 0):
         for k in range(n_blk):
@@ -339,46 +350,32 @@
         near_part(1, k).wait_recv()
         pair_sum[:, at] = acc[pl.ds(pl.multiple_of(far * rows, rows), rows), at] + near_sum[1, :, at]
         far_part(k).start()
-    for i in range(1, N_COL * N_ROW):
-        stat_copy(i).wait_send()
-    for i in (3, 2, 1):
-        x_copy(i).wait_send()
+    count = [sum(KINDS[i % len(KINDS)] == kind for i in range(n_chunks)) for kind in range(3)]
+    done(stats.at[pl.ds(0, N_COL * N_ROW - 1)], s_send.at[0])
 
     @pl.when(is_root)
     def _():
-        for i in (3, 2, 1):
-            g_copy(i).wait_send()
+        done(gain.at[pl.ds(0, N_COL - 1)], g_send.at[0])
+        done(x_all.at[pl.ds(0, (N_ROW - 1) * rows)], x_send.at[0])
+        done(part.at[pl.ds(0, count[1] + count[2])], p_send.at[0])
+        done(part.at[pl.ds(0, count[0] + count[1])], h_send.at[0])
 
     @pl.when(jnp.logical_not(is_root))
     def _():
-        x_copy(0).wait_send()
-
-    def finish(j, _):
-        @pl.when(jnp.logical_not(ends(j)))
-        def _():
-            near_copy(j).wait_send()
-
-        @pl.when(jnp.logical_and(is_root, jnp.logical_not(direct(j))))
-        def _():
-            inner_copy(j).wait_send()
-            outer_copy(j).wait_send()
-
-        @pl.when(jnp.logical_and(forwards, jnp.logical_not(direct(j))))
-        def _():
-            forward_copy(j).wait_send()
-
-        @pl.when(jnp.logical_and(role_last, by_root(j)))
-        def _():
-            last_copy(j, c).wait_send()
-
-        @pl.when(jnp.logical_and(role_last, direct(j)))
-        def _():
-            for to in range(N_COL):
-                last_copy(j, to).wait_send()
-
-        return 0
-
-    lax.fori_loop(0, n_chunks, finish, 0)
+        done(x_all, x_send.at[0])
+
+    @pl.when(role_last)
+    def _():
+        done(part.at[pl.ds(0, count[0])], p_send.at[0])
+        done(part.at[pl.ds(0, (count[1] + N_COL * count[2]) // 2)], w_send.at[0])
+
+    @pl.when(jnp.logical_or(role_near, role_far))
+    def _():
+        done(part, p_send.at[0])
+
+    @pl.when(forwards)
+    def _():
+        done(hid.at[pl.ds(0, count[0] + count[1])], h_send.at[0])
 
     for k in range(n_blk):
         at = pl.ds(k * blk, blk)
@@ -388,12 +385,9 @@
         y_ref[:, at] = (x_own[:, at].astype(F32) + own).astype(BF16)
         store(k).start()
 
-    for i in (1, 0):
-        for k in range(n_blk):
-            near_part(i, k).wait_send()
-    for k in range(n_blk):
-        far_part(k).wait_send()
-        store(k).wait()
+    done(near_sum, n_send.at[0])
+    done(pair_sum, o_send.at[0])
+    done(y_ref, y_store.at[0])
 
 
 def solution(mesh):
@@ -427,11 +421,11 @@
                 pltpu.VMEM((rows, depth), F32),
                 pltpu.VMEM((rows, depth), F32),
                 pltpu.VMEM((rows, depth), BF16),
-                dma((2,)), dma((n_slots,)),
-                dma((N_COL,)), dma((N_ROW,)), dma((N_COL,)), dma((1,)), dma((n_all,)), dma((n_all,)),
-                dma((n_chunks,)), dma((n_chunks,)), dma((n_chunks,)),
-                dma((n_chunks,)), dma((n_chunks,)), dma((n_chunks,)), dma((N_COL, n_chunks)),
-                dma((2, depth // blk)), dma((2, depth // blk)), dma((depth // blk,)), dma((depth // blk,)), dma((depth // blk,)),
+                dma((2,)), dma((n_chunks // 4 + 2,)),
+                dma((1,)), dma((1,)), dma((1,)), dma((1,)), dma((1,)), dma((1,)),
+                dma((1,)), dma((n_chunks,)), dma((n_chunks,)),
+                dma((1,)), dma((n_chunks,)), dma((1,)),
+                dma((1,)), dma((2, depth // blk)), dma((1,)), dma((depth // blk,)), dma((1,)),
             ],
             compiler_params=pltpu.CompilerParams(
                 collective_id=0, has_side_effects=True, vmem_limit_bytes=67_000_000

time: 57.7 us -> 54.7 us (0.948)
  Pallas kernels: 56.1 us -> 53.1 us
    pallas_call x1, Pallas kernels: 56.1 us -> 53.1 us  [local_block(): pl.pallas_call(functools.partial(mlp_kernel, n_chunks, n_slots, blk), out...]
where the time goes in v6:
time: 54.7 us; the launch traced here: 54.6 us
  Pallas kernels  53.1 us (97%)
  local copies, waits for them, and re-layouts  1.47 us (3%)
    pallas_call x1, Pallas kernels, local_block(): pl.pallas_call(functools.partial(mlp_kernel, n_chunks, n_slots, blk), out...  53.1 us
    unnamed x1, local copies, waits for them, and re-layouts  1.47 us

profile of v6, /device:TPU:0, one launch (start us, length us, event | category | flops | bytes accessed | tf_op | source)
XLA Modules:
  0.0 54.6 jit_solution(11324982913286497940)
XLA Ops:
  0.0 53.1 %shard_map.46 = bf16[16,2048]{1,0:T(8,128)(2,1)} custom-call(bf16[16,2048]{1,0:T(8,128)(2,1)} %x_hbm.1, f32[1,2048]{1,0:T(1,128)} %bitcast.1, bf16[2048,8192]{1,0:T(8,128)(2,1)} %w_in_hbm.1, bf16[8192,2048]{1,0:T(8,128)(2,1)} %w_out_hbm.1), custom_call_target="tpu_custom_call" | custom-call | tf_op jit(solution)/shard_map/pallas_call | solution.py:402
  53.1 1.5 %copy.6 = bf16[16,2048]{1,0:T(8,128)(2,1)} copy(bf16[16,2048]{1,0:T(8,128)(2,1)} %shard_map.46) | data formatting | bytes 131072

commit v7 on v6

--- a/solution.py
+++ b/solution.py
@@ -12,7 +12,7 @@
 BF16, F32 = jnp.bfloat16, jnp.float32
 N_COL = 4
 N_ROW = 4
-KINDS = (0, 1, 0, 1, 0, 2, 0, 1, 0, 2, 0, 1, 0, 2, 2, 2)
+KINDS = (0, 1, 0, 1, 0, 1, 0, 1, 0, 0, 0, 2, 2, 2, 2, 2)
 
 
 def gelu_tanh(x):

time: 54.7 us -> 54.9 us (level)
  no operation moved by 1% of the time
where the time goes in v7:
time: 54.9 us; the launch traced here: 54.8 us
  Pallas kernels  53.3 us (97%)
  local copies, waits for them, and re-layouts  1.47 us (3%)
    pallas_call x1, Pallas kernels, local_block(): pl.pallas_call(functools.partial(mlp_kernel, n_chunks, n_slots, blk), out...  53.3 us
    unnamed x1, local copies, waits for them, and re-layouts  1.47 us

profile of v7, /device:TPU:0, one launch (start us, length us, event | category | flops | bytes accessed | tf_op | source)
XLA Modules:
  0.0 54.8 jit_solution(11124390815589994454)
XLA Ops:
  0.0 53.3 %shard_map.46 = bf16[16,2048]{1,0:T(8,128)(2,1)} custom-call(bf16[16,2048]{1,0:T(8,128)(2,1)} %x_hbm.1, f32[1,2048]{1,0:T(1,128)} %bitcast.1, bf16[2048,8192]{1,0:T(8,128)(2,1)} %w_in_hbm.1, bf16[8192,2048]{1,0:T(8,128)(2,1)} %w_out_hbm.1), custom_call_target="tpu_custom_call" | custom-call | tf_op jit(solution)/shard_map/pallas_call | solution.py:402
  53.3 1.5 %copy.6 = bf16[16,2048]{1,0:T(8,128)(2,1)} copy(bf16[16,2048]{1,0:T(8,128)(2,1)} %shard_map.46) | data formatting | bytes 131072

commit v8 on v7

--- a/solution.py
+++ b/solution.py
@@ -252,9 +252,9 @@
 
     acc[...] = jnp.zeros_like(acc)
     behind = 3
-    lag = jnp.where(is_root, 1, jnp.where(role_last, jnp.where(inside, n_chunks // 2, n_chunks), 0))
+    lag = jnp.where(is_root, 1, jnp.where(role_last, jnp.where(inside, 8, 9), 0))
     root_lag = jnp.where(is_root, behind, lag + behind)
-    direct_lag = jnp.where(is_root, 4, lag - 4)
+    direct_lag = jnp.where(is_root, 4, lag - jnp.where(inside, 5, 7))
     second_half = jnp.where(is_root, lag, direct_lag) + n_half
     done(ring.at[pl.ds(n_chunks, n_half)], w_load.at[n_chunks // 4])
 
@@ -324,7 +324,7 @@
         take(t - root_lag, by_root)
         return 0
 
-    lax.fori_loop(0, 2 * n_chunks + behind, step, 0)
+    lax.fori_loop(0, n_chunks + 9 + behind, step, 0)
 
     def near_part(i, k):
         other = near if i == 0 else (near + 2) % N_ROW

time: 54.9 us -> 57 us (1.038)
  Pallas kernels: 53.3 us -> 55.3 us
    pallas_call x1, Pallas kernels: 53.3 us -> 55.3 us  [local_block(): pl.pallas_call(functools.partial(mlp_kernel, n_chunks, n_slots, blk), out...]
where the time goes in v8:
time: 57 us; the launch traced here: 56.8 us
  Pallas kernels  55.3 us (97%)
  local copies, waits for them, and re-layouts  1.47 us (3%)
    pallas_call x1, Pallas kernels, local_block(): pl.pallas_call(functools.partial(mlp_kernel, n_chunks, n_slots, blk), out...  55.3 us
    unnamed x1, local copies, waits for them, and re-layouts  1.47 us

profile of v8, /device:TPU:0, one launch (start us, length us, event | category | flops | bytes accessed | tf_op | source)
XLA Modules:
  0.0 56.8 jit_solution(1580989863212073379)
XLA Ops:
  0.0 55.3 %shard_map.46 = bf16[16,2048]{1,0:T(8,128)(2,1)} custom-call(bf16[16,2048]{1,0:T(8,128)(2,1)} %x_hbm.1, f32[1,2048]{1,0:T(1,128)} %bitcast.1, bf16[2048,8192]{1,0:T(8,128)(2,1)} %w_in_hbm.1, bf16[8192,2048]{1,0:T(8,128)(2,1)} %w_out_hbm.1), custom_call_target="tpu_custom_call" | custom-call | tf_op jit(solution)/shard_map/pallas_call | solution.py:402
  55.3 1.5 %copy.6 = bf16[16,2048]{1,0:T(8,128)(2,1)} copy(bf16[16,2048]{1,0:T(8,128)(2,1)} %shard_map.46) | data formatting | bytes 131072

commit v9 on v6

--- a/solution.py
+++ b/solution.py
@@ -54,17 +54,26 @@
         pc, pr = peer(i)
         pl.semaphore_signal(barrier, inc=1, device_id=(dp, pc, pr), device_id_type=MESH)
 
+    tiles = blk // 128
+
     def load_in(j, slot):
-        pltpu.make_async_copy(
-            w_in_hbm.at[:, pl.ds(pl.multiple_of(j * blk, blk), blk)], ring.at[slot], w_load.at[j // 4]
-        ).start()
+        for k in range(tiles):
+            pltpu.make_async_copy(
+                w_in_hbm.at[:, pl.ds(pl.multiple_of(j * blk + k * 128, 128), 128)],
+                ring.at[slot, k], w_load.at[j // 4],
+            ).start()
 
     def load_out(j, slot):
         for k in range(n_blk):
-            pltpu.make_async_copy(
-                w_out_hbm.at[pl.ds(pl.multiple_of(j * blk, blk), blk), pl.ds(k * blk, blk)],
-                ring.at[slot, pl.ds(k * blk, blk)], w_load.at[n_chunks // 4 + j // n_half],
-            ).start()
+            for m in range(tiles):
+                pltpu.make_async_copy(
+                    w_out_hbm.at[pl.ds(pl.multiple_of(j * blk, blk), blk), pl.ds(k * blk + m * 128, 128)],
+                    ring.at[slot, m, pl.ds(k * blk, blk)], w_load.at[n_chunks // 4 + j // n_half],
+                ).start()
+
+    def weights(slot, k):
+        at = pl.ds(k * blk, blk)
+        return jnp.concatenate([ring[slot, m, at] for m in range(tiles)], axis=1)
 
     n_half = n_chunks // 2
 
@@ -196,10 +205,9 @@
             far_copy(j).start()
 
     def product(j):
-        total = jnp.dot(z_ref[:, pl.ds(0, blk)], ring[j, pl.ds(0, blk)], preferred_element_type=F32)
+        total = jnp.dot(z_ref[:, pl.ds(0, blk)], weights(j, 0), preferred_element_type=F32)
         for k in range(1, n_blk):
-            at = pl.ds(k * blk, blk)
-            total += jnp.dot(z_ref[:, at], ring[j, at], preferred_element_type=F32)
+            total += jnp.dot(z_ref[:, pl.ds(k * blk, blk)], weights(j, k), preferred_element_type=F32)
         return total
 
     def up(i, _):
@@ -301,7 +309,7 @@
         slot = (n_chunks + j) % n_slots
         for k in range(n_blk):
             at = pl.ds(k * blk, blk)
-            acc[:, at] += jnp.dot(hid[j], ring[slot, at], preferred_element_type=F32)
+            acc[:, at] += jnp.dot(hid[j], weights(slot, k), preferred_element_type=F32)
 
     def take(j, wanted):
         @pl.when(jnp.logical_and(j >= 0, j < n_chunks))
@@ -410,7 +418,7 @@
                 pltpu.VMEM((n_all, 1, 128), F32),
                 pltpu.VMEM((tokens, depth), BF16),
                 pltpu.VMEM((tokens, depth), BF16),
-                pltpu.VMEM((n_slots, depth, blk), BF16),
+                pltpu.VMEM((n_slots, blk // 128, depth, 128), BF16),
                 pltpu.VMEM((n_chunks, tokens, blk), F32),
                 pltpu.VMEM((n_chunks, tokens, blk), F32),
                 pltpu.VMEM((n_chunks, tokens, blk), F32),

time: 54.7 us -> 56.1 us (1.026)
  Pallas kernels: 53.1 us -> 54.4 us
    pallas_call x1, Pallas kernels: 53.1 us -> 54.4 us  [local_block(): pl.pallas_call(functools.partial(mlp_kernel, n_chunks, n_slots, blk), out...]
where the time goes in v9:
time: 56.1 us; the launch traced here: 55.9 us
  Pallas kernels  54.4 us (97%)
  local copies, waits for them, and re-layouts  1.47 us (3%)
    pallas_call x1, Pallas kernels, local_block(): pl.pallas_call(functools.partial(mlp_kernel, n_chunks, n_slots, blk), out...  54.4 us
    unnamed x1, local copies, waits for them, and re-layouts  1.47 us

profile of v9, /device:TPU:0, one launch (start us, length us, event | category | flops | bytes accessed | tf_op | source)
XLA Modules:
  0.0 55.9 jit_solution(7002931342401594858)
XLA Ops:
  0.0 54.4 %shard_map.46 = bf16[16,2048]{1,0:T(8,128)(2,1)} custom-call(bf16[16,2048]{1,0:T(8,128)(2,1)} %x_hbm.1, f32[1,2048]{1,0:T(1,128)} %bitcast.1, bf16[2048,8192]{1,0:T(8,128)(2,1)} %w_in_hbm.1, bf16[8192,2048]{1,0:T(8,128)(2,1)} %w_out_hbm.1), custom_call_target="tpu_custom_call" | custom-call | tf_op jit(solution)/shard_map/pallas_call | solution.py:410
  54.4 1.5 %copy.6 = bf16[16,2048]{1,0:T(8,128)(2,1)} copy(bf16[16,2048]{1,0:T(8,128)(2,1)} %shard_map.46) | data formatting | bytes 131072

commit v10 on v7

--- a/solution.py
+++ b/solution.py
@@ -12,7 +12,7 @@
 BF16, F32 = jnp.bfloat16, jnp.float32
 N_COL = 4
 N_ROW = 4
-KINDS = (0, 1, 0, 1, 0, 1, 0, 1, 0, 0, 0, 2, 2, 2, 2, 2)
+KINDS = (0, 1, 0, 0, 1, 0, 2, 0, 0, 1, 0, 2, 0, 1, 0, 2)
 
 
 def gelu_tanh(x):

time: 54.9 us -> 56.3 us (1.026)
  Pallas kernels: 53.3 us -> 54.7 us
    pallas_call x1, Pallas kernels: 53.3 us -> 54.7 us  [local_block(): pl.pallas_call(functools.partial(mlp_kernel, n_chunks, n_slots, blk), out...]
where the time goes in v10:
time: 56.3 us; the launch traced here: 56.2 us
  Pallas kernels  54.7 us (97%)
  local copies, waits for them, and re-layouts  1.47 us (3%)
    pallas_call x1, Pallas kernels, local_block(): pl.pallas_call(functools.partial(mlp_kernel, n_chunks, n_slots, blk), out...  54.7 us
    unnamed x1, local copies, waits for them, and re-layouts  1.47 us

profile of v10, /device:TPU:0, one launch (start us, length us, event | category | flops | bytes accessed | tf_op | source)
XLA Modules:
  0.0 56.2 jit_solution(1223384254406268709)
XLA Ops:
  0.0 54.7 %shard_map.46 = bf16[16,2048]{1,0:T(8,128)(2,1)} custom-call(bf16[16,2048]{1,0:T(8,128)(2,1)} %x_hbm.1, f32[1,2048]{1,0:T(1,128)} %bitcast.1, bf16[2048,8192]{1,0:T(8,128)(2,1)} %w_in_hbm.1, bf16[8192,2048]{1,0:T(8,128)(2,1)} %w_out_hbm.1), custom_call_target="tpu_custom_call" | custom-call | tf_op jit(solution)/shard_map/pallas_call | solution.py:402
  54.7 1.5 %copy.6 = bf16[16,2048]{1,0:T(8,128)(2,1)} copy(bf16[16,2048]{1,0:T(8,128)(2,1)} %shard_map.46) | data formatting | bytes 131072

commit v11 on v7

--- a/solution.py
+++ b/solution.py
@@ -254,8 +254,8 @@
     behind = 3
     lag = jnp.where(is_root, 1, jnp.where(role_last, jnp.where(inside, n_chunks // 2, n_chunks), 0))
     root_lag = jnp.where(is_root, behind, lag + behind)
-    direct_lag = jnp.where(is_root, 4, lag - 4)
-    second_half = jnp.where(is_root, lag, direct_lag) + n_half
+    direct_lag = jnp.where(is_root, 4, lag - jnp.where(inside, 4, 8))
+    second_half = jnp.where(is_root, lag, direct_lag + 2) + n_half
     done(ring.at[pl.ds(n_chunks, n_half)], w_load.at[n_chunks // 4])
 
     def finish_sum(j):

time: 54.9 us -> 53.8 us (0.980)
  Pallas kernels: 53.3 us -> 52.1 us
    pallas_call x1, Pallas kernels: 53.3 us -> 52.1 us  [local_block(): pl.pallas_call(functools.partial(mlp_kernel, n_chunks, n_slots, blk), out...]
where the time goes in v11:
time: 53.8 us; the launch traced here: 53.6 us
  Pallas kernels  52.1 us (97%)
  local copies, waits for them, and re-layouts  1.47 us (3%)
    pallas_call x1, Pallas kernels, local_block(): pl.pallas_call(functools.partial(mlp_kernel, n_chunks, n_slots, blk), out...  52.1 us
    unnamed x1, local copies, waits for them, and re-layouts  1.47 us

profile of v11, /device:TPU:0, one launch (start us, length us, event | category | flops | bytes accessed | tf_op | source)
XLA Modules:
  0.0 53.6 jit_solution(16587618436222135759)
XLA Ops:
  0.0 52.1 %shard_map.46 = bf16[16,2048]{1,0:T(8,128)(2,1)} custom-call(bf16[16,2048]{1,0:T(8,128)(2,1)} %x_hbm.1, f32[1,2048]{1,0:T(1,128)} %bitcast.1, bf16[2048,8192]{1,0:T(8,128)(2,1)} %w_in_hbm.1, bf16[8192,2048]{1,0:T(8,128)(2,1)} %w_out_hbm.1), custom_call_target="tpu_custom_call" | custom-call | tf_op jit(solution)/shard_map/pallas_call | solution.py:402
  52.1 1.5 %copy.6 = bf16[16,2048]{1,0:T(8,128)(2,1)} copy(bf16[16,2048]{1,0:T(8,128)(2,1)} %shard_map.46) | data formatting | bytes 131072

commit v12 on v11

--- a/solution.py
+++ b/solution.py
@@ -254,8 +254,8 @@
     behind = 3
     lag = jnp.where(is_root, 1, jnp.where(role_last, jnp.where(inside, n_chunks // 2, n_chunks), 0))
     root_lag = jnp.where(is_root, behind, lag + behind)
-    direct_lag = jnp.where(is_root, 4, lag - jnp.where(inside, 4, 8))
-    second_half = jnp.where(is_root, lag, direct_lag + 2) + n_half
+    direct_lag = jnp.where(is_root, 4, lag - jnp.where(inside, 0, 8))
+    second_half = jnp.where(is_root | inside, lag, direct_lag + 2) + n_half
     done(ring.at[pl.ds(n_chunks, n_half)], w_load.at[n_chunks // 4])
 
     def finish_sum(j):

time: 53.8 us -> 53.8 us (level)
  no operation moved by 1% of the time
where the time goes in v12:
time: 53.8 us; the launch traced here: 53.6 us
  Pallas kernels  52.1 us (97%)
  local copies, waits for them, and re-layouts  1.47 us (3%)
    pallas_call x1, Pallas kernels, local_block(): pl.pallas_call(functools.partial(mlp_kernel, n_chunks, n_slots, blk), out...  52.1 us
    unnamed x1, local copies, waits for them, and re-layouts  1.47 us

profile of v12, /device:TPU:0, one launch (start us, length us, event | category | flops | bytes accessed | tf_op | source)
XLA Modules:
  0.0 53.6 jit_solution(3076262891624836672)
XLA Ops:
  0.0 52.1 %shard_map.46 = bf16[16,2048]{1,0:T(8,128)(2,1)} custom-call(bf16[16,2048]{1,0:T(8,128)(2,1)} %x_hbm.1, f32[1,2048]{1,0:T(1,128)} %bitcast.1, bf16[2048,8192]{1,0:T(8,128)(2,1)} %w_in_hbm.1, bf16[8192,2048]{1,0:T(8,128)(2,1)} %w_out_hbm.1), custom_call_target="tpu_custom_call" | custom-call | tf_op jit(solution)/shard_map/pallas_call | solution.py:402
  52.1 1.5 %copy.6 = bf16[16,2048]{1,0:T(8,128)(2,1)} copy(bf16[16,2048]{1,0:T(8,128)(2,1)} %shard_map.46) | data formatting | bytes 131072

commit v13 on v12

--- a/solution.py
+++ b/solution.py
@@ -12,7 +12,7 @@
 BF16, F32 = jnp.bfloat16, jnp.float32
 N_COL = 4
 N_ROW = 4
-KINDS = (0, 1, 0, 1, 0, 1, 0, 1, 0, 0, 0, 2, 2, 2, 2, 2)
+KINDS = (0, 1, 0, 1, 0, 1, 0, 1, 0, 1, 0, 1, 2, 2, 2, 2)
 
 
 def gelu_tanh(x):

time: 53.8 us -> 54.7 us (1.017)
  Pallas kernels: 52.1 us -> 53 us
    pallas_call x1, Pallas kernels: 52.1 us -> 53 us  [local_block(): pl.pallas_call(functools.partial(mlp_kernel, n_chunks, n_slots, blk), out...]
where the time goes in v13:
time: 54.7 us; the launch traced here: 54.5 us
  Pallas kernels  53 us (97%)
  local copies, waits for them, and re-layouts  1.47 us (3%)
    pallas_call x1, Pallas kernels, local_block(): pl.pallas_call(functools.partial(mlp_kernel, n_chunks, n_slots, blk), out...  53 us
    unnamed x1, local copies, waits for them, and re-layouts  1.47 us

profile of v13, /device:TPU:0, one launch (start us, length us, event | category | flops | bytes accessed | tf_op | source)
XLA Modules:
  0.0 54.5 jit_solution(10075277766422081502)
XLA Ops:
  0.0 53.0 %shard_map.46 = bf16[16,2048]{1,0:T(8,128)(2,1)} custom-call(bf16[16,2048]{1,0:T(8,128)(2,1)} %x_hbm.1, f32[1,2048]{1,0:T(1,128)} %bitcast.1, bf16[2048,8192]{1,0:T(8,128)(2,1)} %w_in_hbm.1, bf16[8192,2048]{1,0:T(8,128)(2,1)} %w_out_hbm.1), custom_call_target="tpu_custom_call" | custom-call | tf_op jit(solution)/shard_map/pallas_call | solution.py:402
  53.1 1.5 %copy.6 = bf16[16,2048]{1,0:T(8,128)(2,1)} copy(bf16[16,2048]{1,0:T(8,128)(2,1)} %shard_map.46) | data formatting | bytes 131072

commit v14 on v12

--- a/solution.py
+++ b/solution.py
@@ -251,7 +251,7 @@
         return remote(hid_sent.at[j], hid.at[j], w_send.at[0], h_recv.at[j], to, c)
 
     acc[...] = jnp.zeros_like(acc)
-    behind = 3
+    behind = 2
     lag = jnp.where(is_root, 1, jnp.where(role_last, jnp.where(inside, n_chunks // 2, n_chunks), 0))
     root_lag = jnp.where(is_root, behind, lag + behind)
     direct_lag = jnp.where(is_root, 4, lag - jnp.where(inside, 0, 8))

time: 53.8 us -> 54.3 us (level)
  Pallas kernels: 52.1 us -> 52.7 us
    pallas_call x1, Pallas kernels: 52.1 us -> 52.7 us  [local_block(): pl.pallas_call(functools.partial(mlp_kernel, n_chunks, n_slots, blk), out...]
where the time goes in v14:
time: 54.3 us; the launch traced here: 54.2 us
  Pallas kernels  52.7 us (97%)
  local copies, waits for them, and re-layouts  1.47 us (3%)
    pallas_call x1, Pallas kernels, local_block(): pl.pallas_call(functools.partial(mlp_kernel, n_chunks, n_slots, blk), out...  52.7 us
    unnamed x1, local copies, waits for them, and re-layouts  1.47 us

profile of v14, /device:TPU:0, one launch (start us, length us, event | category | flops | bytes accessed | tf_op | source)
XLA Modules:
  0.0 54.2 jit_solution(4301377170087408087)
XLA Ops:
  0.0 52.7 %shard_map.46 = bf16[16,2048]{1,0:T(8,128)(2,1)} custom-call(bf16[16,2048]{1,0:T(8,128)(2,1)} %x_hbm.1, f32[1,2048]{1,0:T(1,128)} %bitcast.1, bf16[2048,8192]{1,0:T(8,128)(2,1)} %w_in_hbm.1, bf16[8192,2048]{1,0:T(8,128)(2,1)} %w_out_hbm.1), custom_call_target="tpu_custom_call" | custom-call | tf_op jit(solution)/shard_map/pallas_call | solution.py:402
  52.7 1.5 %copy.6 = bf16[16,2048]{1,0:T(8,128)(2,1)} copy(bf16[16,2048]{1,0:T(8,128)(2,1)} %shard_map.46) | data formatting | bytes 131072
